TPU v7x, 32 devices: a 4x4x1 block of a 4x4x8 slice. The times are simulated.
32 devices in a mesh: rep: 1 (over z), data: 4 (over y), stage: 8 (over x, core).
Axes of the slice: x: 4, y: 4, z: 1, core: 2. Of those that a mesh axis runs over, the one named last changes fastest.
The devices are a block of a 4x4x8 slice.
Arguments:
- embeds: bfloat16 [12, 4, 256, 768], P(('rep', 'data'))
- targets: bfloat16 [12, 4, 256, 768], P(('rep', 'data'))
- w_qkv: bfloat16 [8, 3, 12, 64, 768], P(('rep', 'stage'))
- w_out: bfloat16 [8, 12, 64, 768], P(('rep', 'stage'))
- w_up: bfloat16 [8, 768, 3072], P(('rep', 'stage'))
- w_down: bfloat16 [8, 3072, 768], P(('rep', 'stage'))
Outputs:
- output 1: float32 [1], P('rep')
- output 2: float32 [8, 3, 12, 64, 768], P(('rep', 'stage'))
- output 3: float32 [8, 12, 64, 768], P(('rep', 'stage'))
- output 4: float32 [8, 768, 3072], P(('rep', 'stage'))
- output 5: float32 [8, 3072, 768], P(('rep', 'stage'))
- output 6: bfloat16 [12, 4, 256, 768], P(('rep', 'data'))
All inputs are finite; a program needn't handle non-finite values.
Results may differ from a plain program's by a relative error of at most 0.02.
Values are sent between devices in bfloat16 or wider.
A program may use at most 768 MiB of HBM per device.

v0:
```python
import jax
import jax.numpy as jnp
from jax import lax
from jax.sharding import PartitionSpec as P

NORM_EPS = 1e-6


def rms_norm(vals):
    return vals * lax.rsqrt(jnp.mean(vals * vals, axis=-1, keepdims=True) + NORM_EPS)


def gelu_tanh(vals):
    return jax.nn.gelu(vals, approximate=True)


def layer_forward(act_in, w_qkv, w_out, w_up, w_down):
    seq_len = act_in.shape[1]
    scale = w_qkv.shape[2] ** -0.5
    act32 = act_in.astype(jnp.float32)
    normed1 = rms_norm(act32).astype(jnp.bfloat16)
    qkv_proj = jnp.einsum('bsd,thkd->tbhsk', normed1, w_qkv, preferred_element_type=jnp.float32).astype(jnp.bfloat16)
    query = qkv_proj[0]
    keys = qkv_proj[1]
    values = qkv_proj[2]
    scores = jnp.einsum('bhqk,bhsk->bhqs', query, keys, preferred_element_type=jnp.float32) * scale
    causal = lax.broadcasted_iota(jnp.int32, (seq_len, seq_len), 0) >= lax.broadcasted_iota(jnp.int32, (seq_len, seq_len), 1)
    probs32 = jax.nn.softmax(jnp.where(causal, scores, -1e30), axis=-1)
    attn_probs = probs32.astype(jnp.bfloat16)
    context = jnp.einsum('bhqs,bhsk->bhqk', attn_probs, values, preferred_element_type=jnp.float32).astype(jnp.bfloat16)
    attn_out = jnp.einsum('cirl,ile->cre', context, w_out, preferred_element_type=jnp.float32)
    hidden32 = (act32 + attn_out).astype(jnp.bfloat16).astype(jnp.float32)
    normed2 = rms_norm(hidden32).astype(jnp.bfloat16)
    pre_act = jnp.einsum('bsd,df->bsf', normed2, w_up, preferred_element_type=jnp.float32)
    upper = gelu_tanh(pre_act).astype(jnp.bfloat16)
    mlp_out = jnp.einsum('bsf,fd->bsd', upper, w_down, preferred_element_type=jnp.float32)
    layer_out = (hidden32 + mlp_out).astype(jnp.bfloat16)
    saved = (act32, normed1, query, keys, values, probs32, attn_probs, context, hidden32, normed2, pre_act, upper)
    return layer_out, saved


def layer_backward(grad_out, saved, w_qkv, w_out, w_up, w_down):
    act32, normed1, query, keys, values, probs32, attn_probs, context, hidden32, normed2, pre_act, upper = saved
    scale = w_qkv.shape[2] ** -0.5
    d_down = jnp.einsum('bsf,bsd->fd', upper, grad_out, preferred_element_type=jnp.float32)
    d_upper = jnp.einsum('bsd,fd->bsf', grad_out, w_down, preferred_element_type=jnp.float32)
    d_pre = jax.vjp(gelu_tanh, pre_act)[1](d_upper)[0].astype(jnp.bfloat16)
    d_up = jnp.einsum('bsd,bsf->df', normed2, d_pre, preferred_element_type=jnp.float32)
    d_normed2 = jnp.einsum('bsf,df->bsd', d_pre, w_up, preferred_element_type=jnp.float32)
    d_hidden = grad_out.astype(jnp.float32) + jax.vjp(rms_norm, hidden32)[1](d_normed2)[0]
    d_hidden16 = d_hidden.astype(jnp.bfloat16)
    d_out = jnp.einsum('cirl,cre->ile', context, d_hidden16, preferred_element_type=jnp.float32)
    d_context = jnp.einsum('cre,ile->cirl', d_hidden16, w_out, preferred_element_type=jnp.float32).astype(jnp.bfloat16)
    d_probs = jnp.einsum('bhqk,bhsk->bhqs', d_context, values, preferred_element_type=jnp.float32)
    d_values = jnp.einsum('bhqs,bhqk->bhsk', attn_probs, d_context, preferred_element_type=jnp.float32)
    d_scores = (probs32 * (d_probs - jnp.sum(d_probs * probs32, axis=-1, keepdims=True)) * scale).astype(jnp.bfloat16)
    d_query = jnp.einsum('bhqs,bhsk->bhqk', d_scores, keys, preferred_element_type=jnp.float32)
    d_keys = jnp.einsum('bhqs,bhqk->bhsk', d_scores, query, preferred_element_type=jnp.float32)
    d_qkv = jnp.stack([d_query, d_keys, d_values]).astype(jnp.bfloat16)
    d_qkv_w = jnp.einsum('tbhsk,bsd->thkd', d_qkv, normed1, preferred_element_type=jnp.float32)
    d_normed1 = jnp.einsum('tbhsk,thkd->bsd', d_qkv, w_qkv, preferred_element_type=jnp.float32)
    d_act = d_hidden + jax.vjp(rms_norm, act32)[1](d_normed1)[0]
    return d_act.astype(jnp.bfloat16), (d_qkv_w, d_out, d_up, d_down)


def solution(mesh):
    n_stages = mesh.shape['stage']
    n_data = mesh.shape['data']
    next_pairs = [(src, src + 1) for src in range(n_stages - 1)]
    prev_pairs = [(src + 1, src) for src in range(n_stages - 1)]
    act_spec = P(('rep', 'data'))
    weight_spec = P(('rep', 'stage'))

    def per_device(embeds, targets, w_qkv, w_out, w_up, w_down):
        weights = (w_qkv[0], w_out[0], w_up[0], w_down[0])
        n_micro, micro_b, seq_len, width = embeds.shape
        stage_idx = lax.axis_index('stage')
        is_first = stage_idx == 0
        is_last = stage_idx == n_stages - 1
        grad_scale = 1.0 / (n_data * n_micro)
        loss_norm = 1.0 / (n_data * n_micro * micro_b * seq_len * width)

        def run_forward(act_in):
            return layer_forward(act_in, *weights)[0]

        def skip_forward(act_in):
            return jnp.zeros_like(act_in)

        def run_backward(operands):
            act_in, grad_out = operands
            saved = layer_forward(act_in, *weights)[1]
            return layer_backward(grad_out, saved, *weights)

        def skip_backward(operands):
            return jnp.zeros_like(operands[0]), tuple(jnp.zeros(w.shape, jnp.float32) for w in weights)

        def tick_body(tick, carry):
            from_prev, from_next, stash, grad_sums, dx_buf, loss_sum = carry
            fwd_micro = tick - stage_idx
            fwd_valid = (fwd_micro >= 0) & (fwd_micro < n_micro)
            fwd_slot = jnp.clip(fwd_micro, 0, n_micro - 1)
            act_in = jnp.where(is_first, lax.dynamic_index_in_dim(embeds, fwd_slot, 0, keepdims=False), from_prev)
            act_out = lax.cond(fwd_valid, run_forward, skip_forward, act_in)
            kept = lax.dynamic_index_in_dim(stash, fwd_slot, 0, keepdims=False)
            stash = lax.dynamic_update_index_in_dim(stash, jnp.where(fwd_valid, act_in, kept), fwd_slot, 0)
            target_mb = lax.dynamic_index_in_dim(targets, fwd_slot, 0, keepdims=False)
            error_mb = act_out.astype(jnp.float32) - target_mb.astype(jnp.float32)
            loss_mb = 0.5 * jnp.sum(error_mb * error_mb) * loss_norm
            loss_sum = loss_sum + jnp.where(is_last & fwd_valid, loss_mb, 0.0)
            grad_seed = (error_mb * grad_scale).astype(jnp.bfloat16)
            bwd_micro = tick + stage_idx - (2 * n_stages - 2)
            bwd_valid = (bwd_micro >= 0) & (bwd_micro < n_micro)
            bwd_slot = jnp.clip(bwd_micro, 0, n_micro - 1)
            grad_out = jnp.where(is_last, grad_seed, from_next)
            act_saved = lax.dynamic_index_in_dim(stash, bwd_slot, 0, keepdims=False)
            grad_in, layer_grads = lax.cond(bwd_valid, run_backward, skip_backward, (act_saved, grad_out))
            grad_sums = tuple(total + piece for total, piece in zip(grad_sums, layer_grads))
            old_dx = lax.dynamic_index_in_dim(dx_buf, bwd_slot, 0, keepdims=False)
            dx_buf = lax.dynamic_update_index_in_dim(dx_buf, jnp.where(is_first & bwd_valid, grad_in, old_dx), bwd_slot, 0)
            from_prev = lax.ppermute(act_out, 'stage', next_pairs)
            from_next = lax.ppermute(grad_in, 'stage', prev_pairs)
            return from_prev, from_next, stash, grad_sums, dx_buf, loss_sum

        micro_zeros = jnp.zeros((micro_b, seq_len, width), jnp.bfloat16)
        init_carry = (micro_zeros, micro_zeros, jnp.zeros_like(embeds), tuple(jnp.zeros(w.shape, jnp.float32) for w in weights), jnp.zeros_like(embeds), jnp.zeros((), jnp.float32))
        n_ticks = n_micro + 2 * n_stages - 2
        final_carry = lax.fori_loop(0, n_ticks, tick_body, init_carry)
        grad_sums = final_carry[3]
        dx_buf = final_carry[4]
        loss_sum = final_carry[5]
        loss = lax.psum(loss_sum, ('data', 'stage')).reshape(1)
        d_weights = tuple(lax.psum(total, 'data')[None] for total in grad_sums)
        d_embeds = lax.psum(dx_buf, 'stage')
        return (loss,) + d_weights + (d_embeds,)

    return jax.shard_map(per_device, mesh=mesh, in_specs=(act_spec, act_spec, weight_spec, weight_spec, weight_spec, weight_spec), out_specs=(P('rep'), weight_spec, weight_spec, weight_spec, weight_spec, act_spec), check_vma=False)
```

profile of v0, /device:TPU:97, one launch (start us, length us, event | category | flops | bytes accessed | tf_op | source)
XLA Modules:
  0.0 3746.1 jit_solution(17028866767056781169)
XLA Ops:
  19.1 3147.7 %while.32 = (s32[]{:T(128)}, bf16[4,256,768]{2,1,0:T(8,128)(2,1)}, bf16[4,256,768]{2,1,0:T(8,128)(2,1)}, bf16[3,4,256,768]{3,2,1,0:T(8,128)(2,1)}, f32[3,12,64,7...) while((s32[]{:T(128)}, bf16[4,256,768]{2,1,0:T(8,128)(2,1)}, ...), condition=%wide.region_17.18_spmd.clone, body=%wide.region_0.17_spmd.clone.sunk | while | flops 56681463808 | bytes 855043136 | solution.py:127
  58.0 36.8 collective-permute-start.1
  135.4 40.5 %conditional.6 = (bf16[4,256,768]{2,1,0:T(8,128)(2,1)}, f32[4,256,768]{2,1,0:T(8,128)S(1)}) conditional(s32[]{:T(128)} %convert_element_type.290, () %tuple.86, (bf16[4,256,768]{2,1,0:T(8,128)(2,1)S(1)}, bf16[3,12,64,768]{3,2,0,1:T(8,128)(2,1)S(1)}, bf16[12,64,768]{2,1,0:T(8,128)(2,1)}, bf16[768,3072]{1,0:T(8,128)(2,1)}, ...), branch_computations={%region_1.1_spmd, %region_2.6_spmd} | conditional | flops 15372453888 | bytes 122945672 | solution.py:103
  181.0 20.5 conditional.7
  253.5 40.6 %conditional.6 = (bf16[4,256,768]{2,1,0:T(8,128)(2,1)}, f32[4,256,768]{2,1,0:T(8,128)S(1)}) conditional(s32[]{:T(128)} %convert_element_type.290, () %tuple.86, (bf16[4,256,768]{2,1,0:T(8,128)(2,1)S(1)}, bf16[3,12,64,768]{3,2,0,1:T(8,128)(2,1)S(1)}, bf16[12,64,768]{2,1,0:T(8,128)(2,1)}, bf16[768,3072]{1,0:T(8,128)(2,1)}, ...), branch_computations={%region_1.1_spmd, %region_2.6_spmd} | conditional | flops 15372453888 | bytes 122945672 | solution.py:103
  299.5 20.3 conditional.7
  371.3 40.9 %conditional.6 = (bf16[4,256,768]{2,1,0:T(8,128)(2,1)}, f32[4,256,768]{2,1,0:T(8,128)S(1)}) conditional(s32[]{:T(128)} %convert_element_type.290, () %tuple.86, (bf16[4,256,768]{2,1,0:T(8,128)(2,1)S(1)}, bf16[3,12,64,768]{3,2,0,1:T(8,128)(2,1)S(1)}, bf16[12,64,768]{2,1,0:T(8,128)(2,1)}, bf16[768,3072]{1,0:T(8,128)(2,1)}, ...), branch_computations={%region_1.1_spmd, %region_2.6_spmd} | conditional | flops 15372453888 | bytes 122945672 | solution.py:103
  494.8 37.7 %collective-permute-start = (bf16[4,256,768]{2,1,0:T(8,128)(2,1)}, bf16[4,256,768]{2,1,0:T(8,128)(2,1)}, u32[]{:S(2)}, u32[]{:S(2)}) collective-permute-start(bf16[4,256,768]{2,1,0:T(8,128)(2,1)} %get-tuple-element.800), channel_id=1, source_target_pairs={{0,1},{1,2},{2,3},{3,4},{4,5},{5,6},{6,7},{8,9},{9,10},{10,11},{11... | collective-permute-start | bytes 4718600 | tf_op jit(solution)/shard_map/while/body/eval_jaxpr/ppermute | solution.py:120
  618.2 20.5 conditional.7
  704.6 25.8 collective-permute-start
  733.6 20.3 conditional.7
  904.8 25.5 collective-permute-start
  1026.9 20.5 conditional.7
  1102.9 85.3 %collective-permute-start = (bf16[4,256,768]{2,1,0:T(8,128)(2,1)}, bf16[4,256,768]{2,1,0:T(8,128)(2,1)}, u32[]{:S(2)}, u32[]{:S(2)}) collective-permute-start(bf16[4,256,768]{2,1,0:T(8,128)(2,1)} %get-tuple-element.800), channel_id=1, source_target_pairs={{0,1},{1,2},{2,3},{3,4},{4,5},{5,6},{6,7},{8,9},{9,10},{10,11},{11... | collective-permute-start | bytes 4718600 | tf_op jit(solution)/shard_map/while/body/eval_jaxpr/ppermute | solution.py:120
  1191.4 20.3 conditional.7
  1255.4 185.9 %collective-permute-done.1 = bf16[4,256,768]{2,1,0:T(8,128)(2,1)S(1)} collective-permute-done((bf16[4,256,768]{2,1,0:T(8,128)(2,1)}, bf16[4,256,768]{2,1,0:T(8,128)(2,1)S(1)}, u32[]{:S(2)}, u32[]{:S(2)}) %collective-permute-start.1) | collective-permute-done | bytes 1572896 | tf_op jit(solution)/shard_map/while/body/eval_jaxpr/ppermute | solution.py:121
  1453.3 135.6 %collective-permute-start = (bf16[4,256,768]{2,1,0:T(8,128)(2,1)}, bf16[4,256,768]{2,1,0:T(8,128)(2,1)}, u32[]{:S(2)}, u32[]{:S(2)}) collective-permute-start(bf16[4,256,768]{2,1,0:T(8,128)(2,1)} %get-tuple-element.800), channel_id=1, source_target_pairs={{0,1},{1,2},{2,3},{3,4},{4,5},{5,6},{6,7},{8,9},{9,10},{10,11},{11... | collective-permute-start | bytes 4718600 | tf_op jit(solution)/shard_map/while/body/eval_jaxpr/ppermute | solution.py:120
  1655.9 184.4 %collective-permute-done.1 = bf16[4,256,768]{2,1,0:T(8,128)(2,1)S(1)} collective-permute-done((bf16[4,256,768]{2,1,0:T(8,128)(2,1)}, bf16[4,256,768]{2,1,0:T(8,128)(2,1)S(1)}, u32[]{:S(2)}, u32[]{:S(2)}) %collective-permute-start.1) | collective-permute-done | bytes 1572896 | tf_op jit(solution)/shard_map/while/body/eval_jaxpr/ppermute | solution.py:121
  1852.4 150.5 %collective-permute-start = (bf16[4,256,768]{2,1,0:T(8,128)(2,1)}, bf16[4,256,768]{2,1,0:T(8,128)(2,1)}, u32[]{:S(2)}, u32[]{:S(2)}) collective-permute-start(bf16[4,256,768]{2,1,0:T(8,128)(2,1)} %get-tuple-element.800), channel_id=1, source_target_pairs={{0,1},{1,2},{2,3},{3,4},{4,5},{5,6},{6,7},{8,9},{9,10},{10,11},{11... | collective-permute-start | bytes 4718600 | tf_op jit(solution)/shard_map/while/body/eval_jaxpr/ppermute | solution.py:120
  2069.8 155.9 %collective-permute-done.1 = bf16[4,256,768]{2,1,0:T(8,128)(2,1)S(1)} collective-permute-done((bf16[4,256,768]{2,1,0:T(8,128)(2,1)}, bf16[4,256,768]{2,1,0:T(8,128)(2,1)S(1)}, u32[]{:S(2)}, u32[]{:S(2)}) %collective-permute-start.1) | collective-permute-done | bytes 1572896 | tf_op jit(solution)/shard_map/while/body/eval_jaxpr/ppermute | solution.py:121
  2237.8 25.7 collective-permute-start
  2266.6 160.5 %conditional.7 = (bf16[4,256,768]{2,1,0:T(8,128)(2,1)}, f32[3,12,64,768]{3,2,1,0:T(8,128)}, f32[12,64,768]{2,1,0:T(8,128)}, f32[768,3072]{1,0:T(8,128)}, f32[3072,768]{1,0:T(8,128)}) conditional(s32[]{:T(128)} %convert_element_type.291, () %tuple.88, (pred[]{:T(512)}, bf16[4,256,768]{2,1,0:T(8,128)(2,1)S(1)}, bf16[4,256,768]{2,1,0:T(8,128)(2,1)S(1)}, ...), branch_computations={%region_7.7_spmd, %region_8.15_spmd} | conditional | flops 41287778304 | bytes 568517952 | solution.py:116
  2386.9 20.7 fusion.128
  2483.0 25.3 collective-permute-start
  2511.4 160.5 %conditional.7 = (bf16[4,256,768]{2,1,0:T(8,128)(2,1)}, f32[3,12,64,768]{3,2,1,0:T(8,128)}, f32[12,64,768]{2,1,0:T(8,128)}, f32[768,3072]{1,0:T(8,128)}, f32[3072,768]{1,0:T(8,128)}) conditional(s32[]{:T(128)} %convert_element_type.291, () %tuple.88, (pred[]{:T(512)}, bf16[4,256,768]{2,1,0:T(8,128)(2,1)S(1)}, bf16[4,256,768]{2,1,0:T(8,128)(2,1)S(1)}, ...), branch_computations={%region_7.7_spmd, %region_8.15_spmd} | conditional | flops 41287778304 | bytes 568517952 | solution.py:116
  2631.6 20.7 fusion.128
  2735.2 160.6 %conditional.7 = (bf16[4,256,768]{2,1,0:T(8,128)(2,1)}, f32[3,12,64,768]{3,2,1,0:T(8,128)}, f32[12,64,768]{2,1,0:T(8,128)}, f32[768,3072]{1,0:T(8,128)}, f32[3072,768]{1,0:T(8,128)}) conditional(s32[]{:T(128)} %convert_element_type.291, () %tuple.88, (pred[]{:T(512)}, bf16[4,256,768]{2,1,0:T(8,128)(2,1)S(1)}, bf16[4,256,768]{2,1,0:T(8,128)(2,1)S(1)}, ...), branch_computations={%region_7.7_spmd, %region_8.15_spmd} | conditional | flops 41287778304 | bytes 568517952 | solution.py:116
  2855.4 20.7 fusion.128
  2958.2 20.5 conditional.7
  2978.7 143.0 %collective-permute-start.1 = (bf16[4,256,768]{2,1,0:T(8,128)(2,1)}, bf16[4,256,768]{2,1,0:T(8,128)(2,1)S(1)}, u32[]{:S(2)}, u32[]{:S(2)}) collective-permute-start(bf16[4,256,768]{2,1,0:T(8,128)(2,1)} %get-tuple-element.804), channel_id=1, source_target_pairs={{1,0},{2,1},{3,2},{4,3},{5,4},{6,5},{7,6},{9,8},{10,9},{11,10},{12... | collective-permute-start | bytes 4718600 | tf_op jit(solution)/shard_map/while/body/eval_jaxpr/ppermute | solution.py:121
  3167.8 47.1 %psum.42 = f32[1]{0:T(128)} all-reduce(f32[1]{0:T(128)} %bitcast.47), channel_id=1, replica_groups=mesh['rep'=1,'data'=4,'stage'=8] {'data','stage'}, use_global_device_ids=true, to_apply=%region_18.19 | all-reduce | flops 1 | bytes 8 | tf_op jit(solution)/shard_map/psum | solution.py:131
  3235.0 480.5 %all-reduce.6.cloned.1.call-done = (f32[1,3,12,64,768]{4,3,2,1,0:T(8,128)}, f32[1,12,64,768]{3,2,1,0:T(8,128)}, f32[1,768,3072]{2,1,0:T(8,128)}, f32[1,3072,768]{2,1,0:T(8,128)}) async-done(((f32[1,3,12,64,768]{4,3,2,1,0:T(8,128)}, f32[1,12,64,768]{3,2,1,0:T(8,128)}, f32[1,768,3072]{2,1,0:T(8,128)}, f32[1,3072,768]{2,1,0:T(8,128)}), (f32[1,3,12,64,768]{4,3,2,1,0:T(8,128)}, f32[1,12,64,768]{3,2,1,0:T(8,128)}, ...) | async-done | bytes 28311568 | tf_op jit(solution)/shard_map/psum | solution.py:132
  (774 shorter events, 1998.5 us)
Async XLA Ops:
  7.2 3227.8 %all-reduce.4.cloned.1.call-start = ((), (), s32[]{:S(2)}) async-start(), calls=%async_computation | async-start | bytes 9437184 | tf_op jit(solution)/shard_map/psum | solution.py:133
  29.8 98.6 %collective-permute-start = (bf16[4,256,768]{2,1,0:T(8,128)(2,1)}, bf16[4,256,768]{2,1,0:T(8,128)(2,1)}, u32[]{:S(2)}, u32[]{:S(2)}) collective-permute-start(bf16[4,256,768]{2,1,0:T(8,128)(2,1)} %get-tuple-element.800), channel_id=1, source_target_pairs={{0,1},{1,2},{2,3},{3,4},{4,5},{5,6},{6,7},{8,9},{9,10},{10,11},{11... | collective-permute-start | bytes 4718600 | tf_op jit(solution)/shard_map/while/body/eval_jaxpr/ppermute | solution.py:120
  58.0 70.4 %collective-permute-start.1 = (bf16[4,256,768]{2,1,0:T(8,128)(2,1)}, bf16[4,256,768]{2,1,0:T(8,128)(2,1)S(1)}, u32[]{:S(2)}, u32[]{:S(2)}) collective-permute-start(bf16[4,256,768]{2,1,0:T(8,128)(2,1)} %get-tuple-element.804), channel_id=1, source_target_pairs={{1,0},{2,1},{3,2},{4,3},{5,4},{6,5},{7,6},{9,8},{10,9},{11,10},{12... | collective-permute-start | bytes 4718600 | tf_op jit(solution)/shard_map/while/body/eval_jaxpr/ppermute | solution.py:121
  175.9 70.8 %collective-permute-start = (bf16[4,256,768]{2,1,0:T(8,128)(2,1)}, bf16[4,256,768]{2,1,0:T(8,128)(2,1)}, u32[]{:S(2)}, u32[]{:S(2)}) collective-permute-start(bf16[4,256,768]{2,1,0:T(8,128)(2,1)} %get-tuple-element.800), channel_id=1, source_target_pairs={{0,1},{1,2},{2,3},{3,4},{4,5},{5,6},{6,7},{8,9},{9,10},{10,11},{11... | collective-permute-start | bytes 4718600 | tf_op jit(solution)/shard_map/while/body/eval_jaxpr/ppermute | solution.py:120
  201.5 45.3 %collective-permute-start.1 = (bf16[4,256,768]{2,1,0:T(8,128)(2,1)}, bf16[4,256,768]{2,1,0:T(8,128)(2,1)S(1)}, u32[]{:S(2)}, u32[]{:S(2)}) collective-permute-start(bf16[4,256,768]{2,1,0:T(8,128)(2,1)} %get-tuple-element.804), channel_id=1, source_target_pairs={{1,0},{2,1},{3,2},{4,3},{5,4},{6,5},{7,6},{9,8},{10,9},{11,10},{12... | collective-permute-start | bytes 4718600 | tf_op jit(solution)/shard_map/while/body/eval_jaxpr/ppermute | solution.py:121
  294.1 70.7 %collective-permute-start = (bf16[4,256,768]{2,1,0:T(8,128)(2,1)}, bf16[4,256,768]{2,1,0:T(8,128)(2,1)}, u32[]{:S(2)}, u32[]{:S(2)}) collective-permute-start(bf16[4,256,768]{2,1,0:T(8,128)(2,1)} %get-tuple-element.800), channel_id=1, source_target_pairs={{0,1},{1,2},{2,3},{3,4},{4,5},{5,6},{6,7},{8,9},{9,10},{10,11},{11... | collective-permute-start | bytes 4718600 | tf_op jit(solution)/shard_map/while/body/eval_jaxpr/ppermute | solution.py:120
  319.8 45.0 %collective-permute-start.1 = (bf16[4,256,768]{2,1,0:T(8,128)(2,1)}, bf16[4,256,768]{2,1,0:T(8,128)(2,1)S(1)}, u32[]{:S(2)}, u32[]{:S(2)}) collective-permute-start(bf16[4,256,768]{2,1,0:T(8,128)(2,1)} %get-tuple-element.804), channel_id=1, source_target_pairs={{1,0},{2,1},{3,2},{4,3},{5,4},{6,5},{7,6},{9,8},{10,9},{11,10},{12... | collective-permute-start | bytes 4718600 | tf_op jit(solution)/shard_map/while/body/eval_jaxpr/ppermute | solution.py:121
  412.1 70.6 %collective-permute-start = (bf16[4,256,768]{2,1,0:T(8,128)(2,1)}, bf16[4,256,768]{2,1,0:T(8,128)(2,1)}, u32[]{:S(2)}, u32[]{:S(2)}) collective-permute-start(bf16[4,256,768]{2,1,0:T(8,128)(2,1)} %get-tuple-element.800), channel_id=1, source_target_pairs={{0,1},{1,2},{2,3},{3,4},{4,5},{5,6},{6,7},{8,9},{9,10},{10,11},{11... | collective-permute-start | bytes 4718600 | tf_op jit(solution)/shard_map/while/body/eval_jaxpr/ppermute | solution.py:120
  437.8 45.0 %collective-permute-start.1 = (bf16[4,256,768]{2,1,0:T(8,128)(2,1)}, bf16[4,256,768]{2,1,0:T(8,128)(2,1)S(1)}, u32[]{:S(2)}, u32[]{:S(2)}) collective-permute-start(bf16[4,256,768]{2,1,0:T(8,128)(2,1)} %get-tuple-element.804), channel_id=1, source_target_pairs={{1,0},{2,1},{3,2},{4,3},{5,4},{6,5},{7,6},{9,8},{10,9},{11,10},{12... | collective-permute-start | bytes 4718600 | tf_op jit(solution)/shard_map/while/body/eval_jaxpr/ppermute | solution.py:121
  494.8 104.6 %collective-permute-start = (bf16[4,256,768]{2,1,0:T(8,128)(2,1)}, bf16[4,256,768]{2,1,0:T(8,128)(2,1)}, u32[]{:S(2)}, u32[]{:S(2)}) collective-permute-start(bf16[4,256,768]{2,1,0:T(8,128)(2,1)} %get-tuple-element.800), channel_id=1, source_target_pairs={{0,1},{1,2},{2,3},{3,4},{4,5},{5,6},{6,7},{8,9},{9,10},{10,11},{11... | collective-permute-start | bytes 4718600 | tf_op jit(solution)/shard_map/while/body/eval_jaxpr/ppermute | solution.py:120
  555.8 43.6 %collective-permute-start.1 = (bf16[4,256,768]{2,1,0:T(8,128)(2,1)}, bf16[4,256,768]{2,1,0:T(8,128)(2,1)S(1)}, u32[]{:S(2)}, u32[]{:S(2)}) collective-permute-start(bf16[4,256,768]{2,1,0:T(8,128)(2,1)} %get-tuple-element.804), channel_id=1, source_target_pairs={{1,0},{2,1},{3,2},{4,3},{5,4},{6,5},{7,6},{9,8},{10,9},{11,10},{12... | collective-permute-start | bytes 4718600 | tf_op jit(solution)/shard_map/while/body/eval_jaxpr/ppermute | solution.py:121
  611.5 70.8 %collective-permute-start = (bf16[4,256,768]{2,1,0:T(8,128)(2,1)}, bf16[4,256,768]{2,1,0:T(8,128)(2,1)}, u32[]{:S(2)}, u32[]{:S(2)}) collective-permute-start(bf16[4,256,768]{2,1,0:T(8,128)(2,1)} %get-tuple-element.800), channel_id=1, source_target_pairs={{0,1},{1,2},{2,3},{3,4},{4,5},{5,6},{6,7},{8,9},{9,10},{10,11},{11... | collective-permute-start | bytes 4718600 | tf_op jit(solution)/shard_map/while/body/eval_jaxpr/ppermute | solution.py:120
  638.7 54.0 %collective-permute-start.1 = (bf16[4,256,768]{2,1,0:T(8,128)(2,1)}, bf16[4,256,768]{2,1,0:T(8,128)(2,1)S(1)}, u32[]{:S(2)}, u32[]{:S(2)}) collective-permute-start(bf16[4,256,768]{2,1,0:T(8,128)(2,1)} %get-tuple-element.804), channel_id=1, source_target_pairs={{1,0},{2,1},{3,2},{4,3},{5,4},{6,5},{7,6},{9,8},{10,9},{11,10},{12... | collective-permute-start | bytes 4718600 | tf_op jit(solution)/shard_map/while/body/eval_jaxpr/ppermute | solution.py:121
  704.6 92.9 %collective-permute-start = (bf16[4,256,768]{2,1,0:T(8,128)(2,1)}, bf16[4,256,768]{2,1,0:T(8,128)(2,1)}, u32[]{:S(2)}, u32[]{:S(2)}) collective-permute-start(bf16[4,256,768]{2,1,0:T(8,128)(2,1)} %get-tuple-element.800), channel_id=1, source_target_pairs={{0,1},{1,2},{2,3},{3,4},{4,5},{5,6},{6,7},{8,9},{9,10},{10,11},{11... | collective-permute-start | bytes 4718600 | tf_op jit(solution)/shard_map/while/body/eval_jaxpr/ppermute | solution.py:120
  753.9 43.6 %collective-permute-start.1 = (bf16[4,256,768]{2,1,0:T(8,128)(2,1)}, bf16[4,256,768]{2,1,0:T(8,128)(2,1)S(1)}, u32[]{:S(2)}, u32[]{:S(2)}) collective-permute-start(bf16[4,256,768]{2,1,0:T(8,128)(2,1)} %get-tuple-element.804), channel_id=1, source_target_pairs={{1,0},{2,1},{3,2},{4,3},{5,4},{6,5},{7,6},{9,8},{10,9},{11,10},{12... | collective-permute-start | bytes 4718600 | tf_op jit(solution)/shard_map/while/body/eval_jaxpr/ppermute | solution.py:121
  809.5 70.6 %collective-permute-start = (bf16[4,256,768]{2,1,0:T(8,128)(2,1)}, bf16[4,256,768]{2,1,0:T(8,128)(2,1)}, u32[]{:S(2)}, u32[]{:S(2)}) collective-permute-start(bf16[4,256,768]{2,1,0:T(8,128)(2,1)} %get-tuple-element.800), channel_id=1, source_target_pairs={{0,1},{1,2},{2,3},{3,4},{4,5},{5,6},{6,7},{8,9},{9,10},{10,11},{11... | collective-permute-start | bytes 4718600 | tf_op jit(solution)/shard_map/while/body/eval_jaxpr/ppermute | solution.py:120
  836.5 56.3 %collective-permute-start.1 = (bf16[4,256,768]{2,1,0:T(8,128)(2,1)}, bf16[4,256,768]{2,1,0:T(8,128)(2,1)S(1)}, u32[]{:S(2)}, u32[]{:S(2)}) collective-permute-start(bf16[4,256,768]{2,1,0:T(8,128)(2,1)} %get-tuple-element.804), channel_id=1, source_target_pairs={{1,0},{2,1},{3,2},{4,3},{5,4},{6,5},{7,6},{9,8},{10,9},{11,10},{12... | collective-permute-start | bytes 4718600 | tf_op jit(solution)/shard_map/while/body/eval_jaxpr/ppermute | solution.py:121
  904.8 92.4 %collective-permute-start = (bf16[4,256,768]{2,1,0:T(8,128)(2,1)}, bf16[4,256,768]{2,1,0:T(8,128)(2,1)}, u32[]{:S(2)}, u32[]{:S(2)}) collective-permute-start(bf16[4,256,768]{2,1,0:T(8,128)(2,1)} %get-tuple-element.800), channel_id=1, source_target_pairs={{0,1},{1,2},{2,3},{3,4},{4,5},{5,6},{6,7},{8,9},{9,10},{10,11},{11... | collective-permute-start | bytes 4718600 | tf_op jit(solution)/shard_map/while/body/eval_jaxpr/ppermute | solution.py:120
  953.6 43.6 %collective-permute-start.1 = (bf16[4,256,768]{2,1,0:T(8,128)(2,1)}, bf16[4,256,768]{2,1,0:T(8,128)(2,1)S(1)}, u32[]{:S(2)}, u32[]{:S(2)}) collective-permute-start(bf16[4,256,768]{2,1,0:T(8,128)(2,1)} %get-tuple-element.804), channel_id=1, source_target_pairs={{1,0},{2,1},{3,2},{4,3},{5,4},{6,5},{7,6},{9,8},{10,9},{11,10},{12... | collective-permute-start | bytes 4718600 | tf_op jit(solution)/shard_map/while/body/eval_jaxpr/ppermute | solution.py:121
  1009.4 81.6 %collective-permute-start = (bf16[4,256,768]{2,1,0:T(8,128)(2,1)}, bf16[4,256,768]{2,1,0:T(8,128)(2,1)}, u32[]{:S(2)}, u32[]{:S(2)}) collective-permute-start(bf16[4,256,768]{2,1,0:T(8,128)(2,1)} %get-tuple-element.800), channel_id=1, source_target_pairs={{0,1},{1,2},{2,3},{3,4},{4,5},{5,6},{6,7},{8,9},{9,10},{10,11},{11... | collective-permute-start | bytes 4718600 | tf_op jit(solution)/shard_map/while/body/eval_jaxpr/ppermute | solution.py:120
  1102.9 152.4 %collective-permute-start = (bf16[4,256,768]{2,1,0:T(8,128)(2,1)}, bf16[4,256,768]{2,1,0:T(8,128)(2,1)}, u32[]{:S(2)}, u32[]{:S(2)}) collective-permute-start(bf16[4,256,768]{2,1,0:T(8,128)(2,1)} %get-tuple-element.800), channel_id=1, source_target_pairs={{0,1},{1,2},{2,3},{3,4},{4,5},{5,6},{6,7},{8,9},{9,10},{10,11},{11... | collective-permute-start | bytes 4718600 | tf_op jit(solution)/shard_map/while/body/eval_jaxpr/ppermute | solution.py:120
  1211.7 229.6 %collective-permute-start.1 = (bf16[4,256,768]{2,1,0:T(8,128)(2,1)}, bf16[4,256,768]{2,1,0:T(8,128)(2,1)S(1)}, u32[]{:S(2)}, u32[]{:S(2)}) collective-permute-start(bf16[4,256,768]{2,1,0:T(8,128)(2,1)} %get-tuple-element.804), channel_id=1, source_target_pairs={{1,0},{2,1},{3,2},{4,3},{5,4},{6,5},{7,6},{9,8},{10,9},{11,10},{12... | collective-permute-start | bytes 4718600 | tf_op jit(solution)/shard_map/while/body/eval_jaxpr/ppermute | solution.py:121
  1453.3 202.6 %collective-permute-start = (bf16[4,256,768]{2,1,0:T(8,128)(2,1)}, bf16[4,256,768]{2,1,0:T(8,128)(2,1)}, u32[]{:S(2)}, u32[]{:S(2)}) collective-permute-start(bf16[4,256,768]{2,1,0:T(8,128)(2,1)} %get-tuple-element.800), channel_id=1, source_target_pairs={{0,1},{1,2},{2,3},{3,4},{4,5},{5,6},{6,7},{8,9},{9,10},{10,11},{11... | collective-permute-start | bytes 4718600 | tf_op jit(solution)/shard_map/while/body/eval_jaxpr/ppermute | solution.py:120
  1612.3 228.1 %collective-permute-start.1 = (bf16[4,256,768]{2,1,0:T(8,128)(2,1)}, bf16[4,256,768]{2,1,0:T(8,128)(2,1)S(1)}, u32[]{:S(2)}, u32[]{:S(2)}) collective-permute-start(bf16[4,256,768]{2,1,0:T(8,128)(2,1)} %get-tuple-element.804), channel_id=1, source_target_pairs={{1,0},{2,1},{3,2},{4,3},{5,4},{6,5},{7,6},{9,8},{10,9},{11,10},{12... | collective-permute-start | bytes 4718600 | tf_op jit(solution)/shard_map/while/body/eval_jaxpr/ppermute | solution.py:121
  1852.4 217.4 %collective-permute-start = (bf16[4,256,768]{2,1,0:T(8,128)(2,1)}, bf16[4,256,768]{2,1,0:T(8,128)(2,1)}, u32[]{:S(2)}, u32[]{:S(2)}) collective-permute-start(bf16[4,256,768]{2,1,0:T(8,128)(2,1)} %get-tuple-element.800), channel_id=1, source_target_pairs={{0,1},{1,2},{2,3},{3,4},{4,5},{5,6},{6,7},{8,9},{9,10},{10,11},{11... | collective-permute-start | bytes 4718600 | tf_op jit(solution)/shard_map/while/body/eval_jaxpr/ppermute | solution.py:120
  2026.2 199.5 %collective-permute-start.1 = (bf16[4,256,768]{2,1,0:T(8,128)(2,1)}, bf16[4,256,768]{2,1,0:T(8,128)(2,1)S(1)}, u32[]{:S(2)}, u32[]{:S(2)}) collective-permute-start(bf16[4,256,768]{2,1,0:T(8,128)(2,1)} %get-tuple-element.804), channel_id=1, source_target_pairs={{1,0},{2,1},{3,2},{4,3},{5,4},{6,5},{7,6},{9,8},{10,9},{11,10},{12... | collective-permute-start | bytes 4718600 | tf_op jit(solution)/shard_map/while/body/eval_jaxpr/ppermute | solution.py:121
  2237.8 233.0 %collective-permute-start = (bf16[4,256,768]{2,1,0:T(8,128)(2,1)}, bf16[4,256,768]{2,1,0:T(8,128)(2,1)}, u32[]{:S(2)}, u32[]{:S(2)}) collective-permute-start(bf16[4,256,768]{2,1,0:T(8,128)(2,1)} %get-tuple-element.800), channel_id=1, source_target_pairs={{0,1},{1,2},{2,3},{3,4},{4,5},{5,6},{6,7},{8,9},{9,10},{10,11},{11... | collective-permute-start | bytes 4718600 | tf_op jit(solution)/shard_map/while/body/eval_jaxpr/ppermute | solution.py:120
  2483.0 232.6 %collective-permute-start = (bf16[4,256,768]{2,1,0:T(8,128)(2,1)}, bf16[4,256,768]{2,1,0:T(8,128)(2,1)}, u32[]{:S(2)}, u32[]{:S(2)}) collective-permute-start(bf16[4,256,768]{2,1,0:T(8,128)(2,1)} %get-tuple-element.800), channel_id=1, source_target_pairs={{0,1},{1,2},{2,3},{3,4},{4,5},{5,6},{6,7},{8,9},{9,10},{10,11},{11... | collective-permute-start | bytes 4718600 | tf_op jit(solution)/shard_map/while/body/eval_jaxpr/ppermute | solution.py:120
  2727.7 211.7 %collective-permute-start = (bf16[4,256,768]{2,1,0:T(8,128)(2,1)}, bf16[4,256,768]{2,1,0:T(8,128)(2,1)}, u32[]{:S(2)}, u32[]{:S(2)}) collective-permute-start(bf16[4,256,768]{2,1,0:T(8,128)(2,1)} %get-tuple-element.800), channel_id=1, source_target_pairs={{0,1},{1,2},{2,3},{3,4},{4,5},{5,6},{6,7},{8,9},{9,10},{10,11},{11... | collective-permute-start | bytes 4718600 | tf_op jit(solution)/shard_map/while/body/eval_jaxpr/ppermute | solution.py:120
  2951.5 211.8 %collective-permute-start = (bf16[4,256,768]{2,1,0:T(8,128)(2,1)}, bf16[4,256,768]{2,1,0:T(8,128)(2,1)}, u32[]{:S(2)}, u32[]{:S(2)}) collective-permute-start(bf16[4,256,768]{2,1,0:T(8,128)(2,1)} %get-tuple-element.800), channel_id=1, source_target_pairs={{0,1},{1,2},{2,3},{3,4},{4,5},{5,6},{6,7},{8,9},{9,10},{10,11},{11... | collective-permute-start | bytes 4718600 | tf_op jit(solution)/shard_map/while/body/eval_jaxpr/ppermute | solution.py:120
  2978.7 184.7 %collective-permute-start.1 = (bf16[4,256,768]{2,1,0:T(8,128)(2,1)}, bf16[4,256,768]{2,1,0:T(8,128)(2,1)S(1)}, u32[]{:S(2)}, u32[]{:S(2)}) collective-permute-start(bf16[4,256,768]{2,1,0:T(8,128)(2,1)} %get-tuple-element.804), channel_id=1, source_target_pairs={{1,0},{2,1},{3,2},{4,3},{5,4},{6,5},{7,6},{9,8},{10,9},{11,10},{12... | collective-permute-start | bytes 4718600 | tf_op jit(solution)/shard_map/while/body/eval_jaxpr/ppermute | solution.py:121
  3167.0 548.5 %all-reduce.6.cloned.1.call-start = ((), (), s32[]{:S(2)}) async-start(), calls=%async_computation.1 | async-start | bytes 56623104 | tf_op jit(solution)/shard_map/psum | solution.py:132
  (160 other events, 1114.5 us)
Sparse Core Ops, SparseCore 0:
  3167.1 67.8 all-reduce.3
  3238.3 477.0 all-reduce.5
where the time goes:
time: 3750 us
  waiting for transfers between devices  1050 us (28%)
  other arithmetic  838 us (22%)
  starting transfers between devices  766 us (20%)
  matrix products  521 us (14%)
  local copies, waits for them, and re-layouts  368 us (10%)
  loops' own time  141 us (4%)
  blocking collectives  47.1 us (1%)
    add x68, other arithmetic, tick_body(): total + piece  637 us
    ppermute x17, starting transfers between devices, tick_body(): from_prev = lax.ppermute(act_out, 'stage', next_pairs)  552 us
    ppermute x17, waiting for transfers between devices, tick_body(): from_next = lax.ppermute(grad_in, 'stage', prev_pairs)  549 us
    psum x1, waiting for transfers between devices, per_device(): d_weights = tuple((lax.psum(total, 'data')[None] for total in grad_sums))  481 us
    another operation x102, local copies, waits for them, and re-layouts  248 us
    ppermute x17, starting transfers between devices, tick_body(): from_next = lax.ppermute(grad_in, 'stage', prev_pairs)  213 us
  transfers between devices with their start and end apart: 36, of which 7 were waited for; matrix products, arithmetic and copies ran while one was open for 38% of the time, Pallas kernels for 0%

commit v1 on v0

v1 whole, which is shorter than its diff:
```python
import functools

import jax
import jax.numpy as jnp
from jax import lax
from jax.experimental import pallas as pl
from jax.experimental.pallas import tpu as pltpu
from jax.sharding import PartitionSpec as P

NORM_EPS = 1e-6
LOG2E = 1.4426950408889634
GELU_C = 0.7978845608028654
GELU_A = 0.044715
MESH_ID = pl.DeviceIdType.MESH


def dot_nn(lhs, rhs):
    return lax.dot_general(lhs, rhs, (((1,), (0,)), ((), ())), preferred_element_type=jnp.float32)


def dot_nt(lhs, rhs):
    return lax.dot_general(lhs, rhs, (((1,), (1,)), ((), ())), preferred_element_type=jnp.float32)


def dot_tn(lhs, rhs):
    return lax.dot_general(lhs, rhs, (((0,), (0,)), ((), ())), preferred_element_type=jnp.float32)


def rms_scale(vals):
    return lax.rsqrt(jnp.mean(vals * vals, axis=-1, keepdims=True) + NORM_EPS)


def rms_vjp(vals, cotangent):
    scale = rms_scale(vals)
    inner = jnp.mean(vals * cotangent, axis=-1, keepdims=True)
    return scale * (cotangent - vals * (scale * scale * inner))


def causal_weights(scores_t, col_max, col_inv, scale):
    half = scores_t.shape[0] // 2
    diag = lax.broadcasted_iota(jnp.int32, (half, half), 0) <= lax.broadcasted_iota(jnp.int32, (half, half), 1)
    upper_l = jnp.where(diag, scores_t[:half, :half], -1e30)
    upper_r = scores_t[:half, half:]
    lower_r = jnp.where(diag, scores_t[half:, half:], -1e30)
    fresh = col_max is None
    if fresh:
        max_l = jnp.max(upper_l, axis=0, keepdims=True)
        max_r = jnp.maximum(jnp.max(upper_r, axis=0, keepdims=True), jnp.max(lower_r, axis=0, keepdims=True))
    else:
        max_l, max_r = col_max[:, :half], col_max[:, half:]
    factor = scale * LOG2E
    exp_ul = jnp.exp2((upper_l - max_l) * factor)
    exp_ur = jnp.exp2((upper_r - max_r) * factor)
    exp_lr = jnp.exp2((lower_r - max_r) * factor)
    if fresh:
        inv_l = 1.0 / jnp.sum(exp_ul, axis=0, keepdims=True)
        inv_r = 1.0 / (jnp.sum(exp_ur, axis=0, keepdims=True) + jnp.sum(exp_lr, axis=0, keepdims=True))
        stats = (jnp.concatenate([max_l, max_r], axis=1), jnp.concatenate([inv_l, inv_r], axis=1))
    else:
        inv_l, inv_r = col_inv[:, :half], col_inv[:, half:]
        stats = None
    return (exp_ul * inv_l, exp_ur * inv_r, exp_lr * inv_r), stats


def assemble(blocks, dtype):
    upper_l, upper_r, lower_r = (b.astype(dtype) for b in blocks)
    upper = jnp.concatenate([upper_l, upper_r], axis=1)
    lower = jnp.concatenate([jnp.zeros_like(upper_l), lower_r], axis=1)
    return jnp.concatenate([upper, lower], axis=0)


def forward_layer(dims, act_ref, wqkv, wout, wup, wdown, n1_ref, qkv_ref, stat_ref, ctx_ref, hid_ref, n2_ref, gp_ref, up_ref, out_ref, flush):
    heads, hdim, ffn_tile = dims
    width = heads * hdim
    ffn = wdown.shape[0]
    scale = hdim ** -0.5
    act32 = act_ref[...].astype(jnp.float32)
    normed1 = (act32 * rms_scale(act32)).astype(jnp.bfloat16)
    n1_ref[...] = normed1
    qkv_ref[...] = dot_nt(wqkv[...], normed1).astype(jnp.bfloat16)
    flush(0)

    def head_body(h, carry):
        q_rows = pl.ds(pl.multiple_of(h * hdim, hdim), hdim)
        k_rows = pl.ds(pl.multiple_of(width + h * hdim, hdim), hdim)
        v_rows = pl.ds(pl.multiple_of(2 * width + h * hdim, hdim), hdim)
        scores_t = dot_tn(qkv_ref[k_rows, :], qkv_ref[q_rows, :])
        blocks, stats = causal_weights(scores_t, None, None, scale)
        stat_ref[h, 0:1, :] = stats[0]
        stat_ref[h, 1:2, :] = stats[1]
        ctx_ref[q_rows, :] = dot_nn(qkv_ref[v_rows, :], assemble(blocks, jnp.bfloat16)).astype(jnp.bfloat16)
        return carry

    lax.fori_loop(0, heads, head_body, 0, unroll=True)
    attn = dot_tn(ctx_ref[...], wout[...])
    hid16 = (act_ref[...].astype(jnp.float32) + attn).astype(jnp.bfloat16)
    hid_ref[...] = hid16
    hid32 = hid16.astype(jnp.float32)
    normed2 = (hid32 * rms_scale(hid32)).astype(jnp.bfloat16)
    n2_ref[...] = normed2
    flush(1)
    for tile in range(ffn // ffn_tile):
        cols = pl.ds(tile * ffn_tile, ffn_tile)
        pre = dot_nn(normed2, wup[:, cols])
        gp_ref[:, cols] = pre
        tanh = jnp.tanh(pre * (GELU_C + (GELU_C * GELU_A) * (pre * pre)))
        up_ref[:, cols] = (pre * (0.5 + 0.5 * tanh)).astype(jnp.bfloat16)
    flush(2)
    down = dot_nn(up_ref[...], wdown[...])
    out_ref[...] = (hid_ref[...].astype(jnp.float32) + down).astype(jnp.bfloat16)


def backward_layer(dims, grad_ref, act_ref, wqkv, wout, wup, wdown, qkv_ref, stat_ref, hid_ref, gp_ref, dpre_ref, dhid_ref, dctx_ref, dqkv_ref, dact_ref, flush):
    heads, hdim, ffn_tile = dims
    width = heads * hdim
    ffn = wdown.shape[0]
    scale = hdim ** -0.5
    grad16 = grad_ref[...]
    for tile in range(ffn // ffn_tile):
        cols = pl.ds(tile * ffn_tile, ffn_tile)
        dup = dot_nt(grad16, wdown[cols, :])
        pre = gp_ref[:, cols]
        pre_sq = pre * pre
        tanh = jnp.tanh(pre * (GELU_C + (GELU_C * GELU_A) * pre_sq))
        half = 0.5 + 0.5 * tanh
        bend = (half * (1.0 - half)) * (pre * (2.0 * GELU_C + (6.0 * GELU_C * GELU_A) * pre_sq))
        dpre_ref[:, cols] = (dup * (half + bend)).astype(jnp.bfloat16)
    flush(0)
    dnormed2 = dot_nt(dpre_ref[...], wup[...])
    dhid32 = grad_ref[...].astype(jnp.float32) + rms_vjp(hid_ref[...].astype(jnp.float32), dnormed2)
    dhid16 = dhid32.astype(jnp.bfloat16)
    dhid_ref[...] = dhid16
    flush(1)
    dctx_ref[...] = dot_nt(wout[...], dhid16).astype(jnp.bfloat16)

    def head_body(h, carry):
        q_rows = pl.ds(pl.multiple_of(h * hdim, hdim), hdim)
        k_rows = pl.ds(pl.multiple_of(width + h * hdim, hdim), hdim)
        v_rows = pl.ds(pl.multiple_of(2 * width + h * hdim, hdim), hdim)
        query_t = qkv_ref[q_rows, :]
        keys_t = qkv_ref[k_rows, :]
        dctx_t = dctx_ref[q_rows, :]
        scores_t = dot_tn(keys_t, query_t)
        probs, _ = causal_weights(scores_t, stat_ref[h, 0:1, :], stat_ref[h, 1:2, :], scale)
        dprobs = dot_tn(qkv_ref[v_rows, :], dctx_t)
        half = dprobs.shape[0] // 2
        d_ul, d_ur, d_lr = dprobs[:half, :half], dprobs[:half, half:], dprobs[half:, half:]
        p_ul, p_ur, p_lr = probs
        delta_l = jnp.sum(d_ul * p_ul, axis=0, keepdims=True)
        delta_r = jnp.sum(d_ur * p_ur, axis=0, keepdims=True) + jnp.sum(d_lr * p_lr, axis=0, keepdims=True)
        dscores = assemble((p_ul * (d_ul - delta_l) * scale, p_ur * (d_ur - delta_r) * scale, p_lr * (d_lr - delta_r) * scale), jnp.bfloat16)
        dqkv_ref[v_rows, :] = dot_nt(dctx_t, assemble(probs, jnp.bfloat16)).astype(jnp.bfloat16)
        dqkv_ref[q_rows, :] = dot_nn(keys_t, dscores).astype(jnp.bfloat16)
        dqkv_ref[k_rows, :] = dot_nt(query_t, dscores).astype(jnp.bfloat16)
        return carry

    lax.fori_loop(0, heads, head_body, 0, unroll=True)
    flush(2)
    dnormed1 = dot_tn(dqkv_ref[...], wqkv[...])
    dact = dhid32 + rms_vjp(act_ref[...].astype(jnp.float32), dnormed1)
    dact_ref[...] = dact.astype(jnp.bfloat16)


def pipeline_kernel(
    cfg,
    emb_hbm, tgt_hbm, wqkv_hbm, wout_hbm, wup_hbm, wdown_hbm,
    loss_ref, n1_hbm, n2_hbm, up_hbm, ctx_hbm, dqkv_hbm, dpre_hbm, dhid_hbm, g_hbm, dx_hbm, qkv_hbm, gp_hbm, hid_hbm, stat_hbm,
    wqkv, wout, wup, wdown, act, grad, out_s, dact_s,
    n1_s, n2_s, up_s, ctx_s, qkv_s, gp_s, hid_s, stat_s,
    dpre_s, dhid_s, dctx_s, dqkv_s,
    w_sem, in_sem, act_sem, grad_sem, fout_sem, bin_sem, bout_sem, fsend_sem, bsend_sem, loss_acc, loss_sem,
):
    n_stages, n_seq, tokens, grad_scale, dims = cfg
    stage = lax.axis_index('stage')
    is_first = stage == 0
    is_last = stage == n_stages - 1
    nxt = lax.rem(stage + 1, n_stages)
    prv = lax.rem(stage + n_stages - 1, n_stages)

    weight_pairs = ((wqkv_hbm, wqkv), (wout_hbm, wout), (wup_hbm, wup), (wdown_hbm, wdown))
    for idx, (src, dst) in enumerate(weight_pairs):
        pltpu.make_async_copy(src, dst, w_sem.at[idx]).start()

    def load_embed(m):
        return pltpu.make_async_copy(emb_hbm.at[m], act.at[m], in_sem.at[m])

    def load_target(m):
        return pltpu.make_async_copy(tgt_hbm.at[m], grad.at[m], in_sem.at[m])

    @pl.when(is_first)
    def _():
        def go(m, carry):
            load_embed(m).start()
            return carry
        lax.fori_loop(0, n_seq, go, 0)

    @pl.when(is_last)
    def _():
        def go(m, carry):
            load_target(m).start()
            return carry
        lax.fori_loop(0, n_seq, go, 0)

    barrier = pltpu.get_barrier_semaphore()
    for peer in (prv, nxt):
        pl.semaphore_signal(barrier, inc=1, device_id={'stage': peer}, device_id_type=MESH_ID)
    pl.semaphore_wait(barrier, 2)

    loss_acc[...] = jnp.zeros_like(loss_acc)
    for idx, (src, dst) in enumerate(weight_pairs):
        pltpu.make_async_copy(src, dst, w_sem.at[idx]).wait()

    def send_act(m, slot):
        return pltpu.make_async_remote_copy(
            src_ref=out_s.at[slot], dst_ref=act.at[m], send_sem=fsend_sem.at[slot], recv_sem=act_sem.at[m],
            device_id={'stage': nxt}, device_id_type=MESH_ID)

    def send_grad(m, slot):
        return pltpu.make_async_remote_copy(
            src_ref=dact_s.at[slot], dst_ref=grad.at[m], send_sem=bsend_sem.at[slot], recv_sem=grad_sem.at[m],
            device_id={'stage': prv}, device_id_type=MESH_ID)

    def store_dx(m, slot):
        return pltpu.make_async_copy(dact_s.at[slot], dx_hbm.at[m], bsend_sem.at[slot])

    def token_range(m):
        return pl.ds(pl.multiple_of(m * tokens, tokens), tokens)

    def fout_copies(m, slot):
        rows = token_range(m)
        return (
            (0, pltpu.make_async_copy(n1_s.at[slot], n1_hbm.at[rows, :], fout_sem.at[slot, 0])),
            (0, pltpu.make_async_copy(qkv_s.at[slot], qkv_hbm.at[m], fout_sem.at[slot, 1])),
            (1, pltpu.make_async_copy(ctx_s.at[slot], ctx_hbm.at[:, rows], fout_sem.at[slot, 2])),
            (1, pltpu.make_async_copy(stat_s.at[slot], stat_hbm.at[m], fout_sem.at[slot, 3])),
            (1, pltpu.make_async_copy(hid_s.at[slot], hid_hbm.at[m], fout_sem.at[slot, 4])),
            (1, pltpu.make_async_copy(n2_s.at[slot], n2_hbm.at[rows, :], fout_sem.at[slot, 5])),
            (2, pltpu.make_async_copy(gp_s.at[slot], gp_hbm.at[m], fout_sem.at[slot, 6])),
            (2, pltpu.make_async_copy(up_s.at[slot], up_hbm.at[rows, :], fout_sem.at[slot, 7])),
        )

    def bin_copies(m):
        return (
            pltpu.make_async_copy(qkv_hbm.at[m], qkv_s.at[2], bin_sem.at[0]),
            pltpu.make_async_copy(stat_hbm.at[m], stat_s.at[2], bin_sem.at[1]),
            pltpu.make_async_copy(hid_hbm.at[m], hid_s.at[2], bin_sem.at[2]),
            pltpu.make_async_copy(gp_hbm.at[m], gp_s.at[2], bin_sem.at[3]),
        )

    def bout_copies(m, slot):
        rows = token_range(m)
        return (
            (0, pltpu.make_async_copy(grad.at[m], g_hbm.at[rows, :], bout_sem.at[slot, 0])),
            (0, pltpu.make_async_copy(dpre_s.at[slot], dpre_hbm.at[rows, :], bout_sem.at[slot, 1])),
            (1, pltpu.make_async_copy(dhid_s.at[slot], dhid_hbm.at[rows, :], bout_sem.at[slot, 2])),
            (2, pltpu.make_async_copy(dqkv_s.at[slot], dqkv_hbm.at[:, rows], bout_sem.at[slot, 3])),
        )

    def flusher(copies):
        def flush(group):
            for when, copy in copies:
                if when == group:
                    copy.start()
        return flush

    def in_range(m):
        return (m >= 0) & (m < n_seq)

    def tick(t, carry):
        fwd_m = t - stage
        bwd_m = t + stage - (2 * n_stages - 2)

        @pl.when(in_range(fwd_m))
        def _():
            m = fwd_m
            slot = lax.rem(m, 2)

            @pl.when(is_first)
            def _():
                load_embed(m).wait()

            @pl.when(jnp.logical_not(is_first))
            def _():
                send_act(m, slot).wait_recv()

            forward_layer(
                dims, act.at[m], wqkv, wout, wup, wdown, n1_s.at[slot], qkv_s.at[slot], stat_s.at[slot],
                ctx_s.at[slot], hid_s.at[slot], n2_s.at[slot], gp_s.at[slot], up_s.at[slot], out_s.at[slot],
                flusher(fout_copies(m, slot)))

            @pl.when(jnp.logical_not(is_last))
            def _():
                send_act(m, slot).start()

            @pl.when(is_last)
            def _():
                load_target(m).wait()
                error = out_s[slot].astype(jnp.float32) - grad[m].astype(jnp.float32)
                square = error * error
                total = square[0:8]
                for row in range(8, tokens, 8):
                    total = total + square[row:row + 8]
                loss_acc[...] += total
                grad[m] = (error * grad_scale).astype(jnp.bfloat16)

        @pl.when(in_range(bwd_m))
        def _():
            m = bwd_m
            slot = lax.rem(m, 2)

            @pl.when(jnp.logical_not(is_last))
            def _():
                for copy in bin_copies(m):
                    copy.wait()
                send_grad(m, slot).wait_recv()

            saved = jnp.where(is_last, slot, 2)
            backward_layer(
                dims, grad.at[m], act.at[m], wqkv, wout, wup, wdown, qkv_s.at[saved], stat_s.at[saved], hid_s.at[saved],
                gp_s.at[saved], dpre_s.at[slot], dhid_s.at[slot], dctx_s, dqkv_s.at[slot], dact_s.at[slot],
                flusher(bout_copies(m, slot)))

            @pl.when(jnp.logical_not(is_first))
            def _():
                send_grad(m, slot).start()

            @pl.when(is_first)
            def _():
                store_dx(m, slot).start()

        fwd_old = fwd_m - 1
        bwd_old = bwd_m - 1

        @pl.when(in_range(fwd_old))
        def _():
            slot = lax.rem(fwd_old, 2)
            for _, copy in fout_copies(fwd_old, slot):
                copy.wait()

            @pl.when(jnp.logical_not(is_last))
            def _():
                send_act(fwd_old, slot).wait_send()

        @pl.when(in_range(bwd_old))
        def _():
            slot = lax.rem(bwd_old, 2)
            for _, copy in bout_copies(bwd_old, slot):
                copy.wait()

            @pl.when(jnp.logical_not(is_first))
            def _():
                send_grad(bwd_old, slot).wait_send()

            @pl.when(is_first)
            def _():
                store_dx(bwd_old, slot).wait()

        @pl.when(in_range(bwd_m + 1) & jnp.logical_not(is_last))
        def _():
            for copy in bin_copies(bwd_m + 1):
                copy.start()

        return carry

    lax.fori_loop(0, n_seq + 2 * n_stages - 1, tick, 0)

    def send_loss():
        return pltpu.make_async_remote_copy(
            src_ref=loss_ref, dst_ref=loss_ref, send_sem=loss_sem.at[0], recv_sem=loss_sem.at[1],
            device_id={'stage': prv}, device_id_type=MESH_ID)

    @pl.when(is_last)
    def _():
        lanes = loss_ref.shape[1]
        total = loss_acc[:, 0:lanes]
        for col in range(lanes, loss_acc.shape[1], lanes):
            total = total + loss_acc[:, col:col + lanes]
        loss_ref[...] = total

    @pl.when(jnp.logical_not(is_last))
    def _():
        send_loss().wait_recv()

    @pl.when(jnp.logical_not(is_first))
    def _():
        send_loss().start()
        send_loss().wait_send()


def run_pipeline(n_stages, grad_scale, embeds, targets, wqkv, wout, wup, wdown, heads, hdim):
    n_seq, tokens, width = embeds.shape
    ffn = wdown.shape[0]
    dims = (heads, hdim, 512 if ffn % 512 == 0 else ffn)
    bf16, f32 = jnp.bfloat16, jnp.float32
    total = n_seq * tokens
    out_shapes = [
        ((8, 128), f32),
        ((total, width), bf16),
        ((total, width), bf16),
        ((total, ffn), bf16),
        ((width, total), bf16),
        ((3 * width, total), bf16),
        ((total, ffn), bf16),
        ((total, width), bf16),
        ((total, width), bf16),
        ((n_seq, tokens, width), bf16),
        ((n_seq, 3 * width, tokens), bf16),
        ((n_seq, tokens, ffn), f32),
        ((n_seq, tokens, width), bf16),
        ((n_seq, heads, 8, tokens), f32),
    ]
    any_spec = pl.BlockSpec(memory_space=pl.ANY)
    scratch = [
        pltpu.VMEM(wqkv.shape, bf16), pltpu.VMEM(wout.shape, bf16), pltpu.VMEM(wup.shape, bf16), pltpu.VMEM(wdown.shape, bf16),
        pltpu.VMEM((n_seq, tokens, width), bf16), pltpu.VMEM((n_seq, tokens, width), bf16),
        pltpu.VMEM((2, tokens, width), bf16), pltpu.VMEM((2, tokens, width), bf16),
        pltpu.VMEM((2, tokens, width), bf16), pltpu.VMEM((2, tokens, width), bf16),
        pltpu.VMEM((2, tokens, ffn), bf16), pltpu.VMEM((2, width, tokens), bf16),
        pltpu.VMEM((3, 3 * width, tokens), bf16), pltpu.VMEM((3, tokens, ffn), f32),
        pltpu.VMEM((3, tokens, width), bf16), pltpu.VMEM((3, heads, 8, tokens), f32),
        pltpu.VMEM((2, tokens, ffn), bf16), pltpu.VMEM((2, tokens, width), bf16),
        pltpu.VMEM((width, tokens), bf16), pltpu.VMEM((2, 3 * width, tokens), bf16),
        pltpu.SemaphoreType.DMA((4,)), pltpu.SemaphoreType.DMA((n_seq,)),
        pltpu.SemaphoreType.DMA((n_seq,)), pltpu.SemaphoreType.DMA((n_seq,)),
        pltpu.SemaphoreType.DMA((2, 8)), pltpu.SemaphoreType.DMA((4,)), pltpu.SemaphoreType.DMA((2, 4)),
        pltpu.SemaphoreType.DMA((2,)), pltpu.SemaphoreType.DMA((2,)),
        pltpu.VMEM((8, width), f32), pltpu.SemaphoreType.DMA((2,)),
    ]
    linear = 2 * total * (wqkv.size + wout.size + wup.size + wdown.size)
    return pl.pallas_call(
        functools.partial(pipeline_kernel, (n_stages, n_seq, tokens, grad_scale, dims)),
        out_shape=[jax.ShapeDtypeStruct(s, d) for s, d in out_shapes],
        in_specs=[any_spec] * 6,
        out_specs=[pl.BlockSpec(memory_space=pltpu.VMEM)] + [any_spec] * (len(out_shapes) - 1),
        scratch_shapes=scratch,
        compiler_params=pltpu.CompilerParams(collective_id=0, has_side_effects=True, vmem_limit_bytes=67043328),
        cost_estimate=pl.CostEstimate(flops=3 * linear, bytes_accessed=200 * 2 ** 20, transcendentals=0),
        name='stage_pipeline',
    )(embeds, targets, wqkv, wout, wup, wdown)


def reduce_kernel(
    cfg,
    loss_hbm, ctx_hbm, dhid_hbm, dqkv_hbm, n1_hbm, up_hbm, g_hbm, n2_hbm, dpre_hbm, dx_hbm,
    loss_ref, dout_hbm, dqkvw_hbm, ddown_hbm, dup_hbm, demb_hbm,
    out_res, qkv_res, down_res, up_res, out_in, qkv_in, down_in, up_in, out_sl, qkv_sl, down_sl, up_sl, loss_sl,
    res_sem, in_sem, rs_send, rs_recv, ag_send, ag_recv, store_sem, dx_sem, loss_send, loss_recv, loss_in,
):
    n_data, n_stages = cfg
    rank = lax.axis_index('data')
    stage = lax.axis_index('stage')
    right = lax.rem(rank + 1, n_data)
    left = lax.rem(rank + n_data - 1, n_data)
    toward = (right, left)
    last = n_data - 1

    kinds = (
        ('rows', dhid_hbm, out_res, ctx_hbm, out_in, out_sl, dout_hbm),
        ('rows', n1_hbm, qkv_res, dqkv_hbm, qkv_in, qkv_sl, dqkvw_hbm),
        ('tall', g_hbm, down_res, up_hbm, down_in, down_sl, ddown_hbm),
        ('wide', n2_hbm, up_res, dpre_hbm, up_in, up_sl, dup_hbm),
    )
    order = ((0, 0), (0, 1), (1, 0), (1, 1), (2, 0), (3, 0), (2, 1), (3, 1))

    def owner_of(step, way):
        turn = step + 1
        return lax.rem(rank + (n_data - turn if way == 0 else turn), n_data)

    def piece(kind, way, owner):
        size = kinds[kind][4].shape[1 if kinds[kind][0] == 'rows' else 2]
        return pl.ds(pl.multiple_of((way * n_data + owner) * size, size), size)

    def read_piece(kind, way, step):
        form, _, _, src, buf, _, _ = kinds[kind]
        part = piece(kind, way, owner_of(step, way))
        view = src.at[part, :] if form == 'rows' else src.at[:, part]
        buf_idx = way if buf.shape[0] == 2 else 0
        return pltpu.make_async_copy(view, buf.at[buf_idx], in_sem.at[kind, buf_idx])

    def out_view(kind, way, owner):
        part = piece(kind, way, owner)
        dst = kinds[kind][6]
        return dst.at[:, part] if kinds[kind][0] == 'wide' else dst.at[part, :]

    def pass_sum(kind, way, step):
        slots = kinds[kind][5]
        return pltpu.make_async_remote_copy(
            src_ref=slots.at[step, way], dst_ref=slots.at[step + 1, way], send_sem=rs_send.at[step, kind, way],
            recv_sem=rs_recv.at[step, kind, way], device_id={'data': toward[way]}, device_id_type=MESH_ID)

    def share(kind, way, step):
        owner = lax.rem(rank + (n_data - step if way == 0 else step), n_data)
        view = out_view(kind, way, owner)
        return pltpu.make_async_remote_copy(
            src_ref=kinds[kind][5].at[last, way] if step == 0 else view, dst_ref=view,
            send_sem=ag_send.at[step, kind, way], recv_sem=ag_recv.at[step, kind, way],
            device_id={'data': toward[way]}, device_id_type=MESH_ID)

    def shared_in(kind, way, step):
        owner = lax.rem(rank + (n_data - step - 1 if way == 0 else step + 1), n_data)
        view = out_view(kind, way, owner)
        return pltpu.make_async_remote_copy(
            src_ref=view, dst_ref=view, send_sem=ag_send.at[step, kind, way], recv_sem=ag_recv.at[step, kind, way],
            device_id={'data': toward[way]}, device_id_type=MESH_ID)

    def keep(kind, way):
        return pltpu.make_async_copy(kinds[kind][5].at[last, way], out_view(kind, way, rank), store_sem.at[kind, way])

    def load_resident(kind):
        return pltpu.make_async_copy(kinds[kind][1], kinds[kind][2], res_sem.at[kind])

    my_loss = pltpu.make_async_copy(loss_hbm, loss_sl.at[rank], loss_in)
    my_loss.start()
    for kind in range(len(kinds)):
        load_resident(kind).start()
        for way in range(kinds[kind][4].shape[0]):
            read_piece(kind, way, 0).start()

    spans = []
    span = n_stages // 2
    while span >= 1:
        spans.append(span)
        span //= 2
    barrier = pltpu.get_barrier_semaphore()
    for turn in range(1, n_data):
        pl.semaphore_signal(barrier, inc=1, device_id={'data': lax.rem(rank + turn, n_data)}, device_id_type=MESH_ID)
    for span in spans:
        upper = lax.rem(lax.div(stage, span), 2)
        pl.semaphore_signal(barrier, inc=1, device_id={'stage': stage + span - 2 * span * upper}, device_id_type=MESH_ID)
    pl.semaphore_wait(barrier, n_data - 1 + len(spans))

    def send_loss(turn):
        return pltpu.make_async_remote_copy(
            src_ref=loss_sl.at[rank], dst_ref=loss_sl.at[rank], send_sem=loss_send.at[turn - 1], recv_sem=loss_recv.at[turn - 1],
            device_id={'data': lax.rem(rank + turn, n_data)}, device_id_type=MESH_ID)

    def loss_arrival(turn):
        sender = lax.rem(rank + n_data - turn, n_data)
        return pltpu.make_async_remote_copy(
            src_ref=loss_sl.at[sender], dst_ref=loss_sl.at[sender], send_sem=loss_send.at[turn - 1], recv_sem=loss_recv.at[turn - 1],
            device_id={'data': lax.rem(rank + turn, n_data)}, device_id_type=MESH_ID)

    my_loss.wait()
    for turn in range(1, n_data):
        send_loss(turn).start()

    def spread(idx):
        return pltpu.make_async_remote_copy(
            src_ref=demb_hbm, dst_ref=demb_hbm, send_sem=dx_sem.at[0, idx], recv_sem=dx_sem.at[1, idx],
            device_id={'stage': lax.rem(stage + spans[idx], n_stages)}, device_id_type=MESH_ID)

    def sends_at(idx):
        return lax.rem(stage, 2 * spans[idx]) == 0

    def receives_at(idx):
        return lax.rem(stage, 2 * spans[idx]) == spans[idx]

    def spread_round(idx):
        if idx > 0:
            @pl.when(receives_at(idx - 1))
            def _():
                spread(idx - 1).wait_recv()
        if idx < len(spans):
            @pl.when(sends_at(idx))
            def _():
                spread(idx).start()

    for kind in range(len(kinds)):
        slots = kinds[kind][5]
        for way in range(2):
            slots[0, way] = jnp.zeros(slots.shape[2:], slots.dtype)

    def add_product(kind, way, step):
        form, _, res, _, buf, slots, _ = kinds[kind]
        fed = buf.at[way if buf.shape[0] == 2 else 0]
        tile = min(256, res.shape[1])

        def body(n, carry):
            cols = pl.ds(pl.multiple_of(n * tile, tile), tile)
            if form == 'rows':
                slots[step, way, :, cols] += dot_nn(fed[...], res[:, cols])
            elif form == 'tall':
                slots[step, way, :, cols] += dot_tn(fed[...], res[:, cols])
            else:
                slots[step, way, cols, :] += dot_tn(res[:, cols], fed[...])
            return carry

        lax.fori_loop(0, res.shape[1] // tile, body, 0)

    def ring_step(step, carry):
        for kind, way in order:
            @pl.when(step == 0)
            def _():
                if way == 0:
                    load_resident(kind).wait()

            read_piece(kind, way, step).wait()

            @pl.when(step > 0)
            def _():
                pass_sum(kind, way, step - 1).wait_recv()

            add_product(kind, way, step)
            if kinds[kind][4].shape[0] == 2:
                @pl.when(step < last)
                def _():
                    read_piece(kind, way, step + 1).start()
            elif way == 0:
                read_piece(kind, 1, step).start()
            else:
                @pl.when(step < last)
                def _():
                    read_piece(kind, 0, step + 1).start()

            @pl.when(step < last)
            def _():
                pass_sum(kind, way, step).start()

            @pl.when(step == last)
            def _():
                keep(kind, way).start()
                share(kind, way, 0).start()

        for idx in range(min(last, len(spans))):
            @pl.when(step == idx)
            def _():
                spread_round(idx)
        return carry

    lax.fori_loop(0, n_data, ring_step, 0)

    for idx in range(min(last, len(spans)), len(spans) + 1):
        spread_round(idx)
    for step in range(1, last):
        for kind, way in order:
            shared_in(kind, way, step - 1).wait_recv()
            share(kind, way, step).start()

    for turn in range(1, n_data):
        loss_arrival(turn).wait_recv()
    total = loss_sl[0]
    for idx in range(1, n_data):
        total = total + loss_sl[idx]
    loss_ref[...] = total

    for kind, way in order:
        shared_in(kind, way, last - 1).wait_recv()
    for kind, way in order:
        keep(kind, way).wait()
        for step in range(last):
            pass_sum(kind, way, step).wait_send()
            share(kind, way, step).wait_send()
    for turn in range(1, n_data):
        send_loss(turn).wait_send()
    for idx in range(len(spans)):
        @pl.when(sends_at(idx))
        def _():
            spread(idx).wait_send()


def sum_gradients(n_data, n_stages, loss_part, ctx_t, dhid, dqkv_t, n1, upper, grads, n2, dpre, dx):
    bf16, f32 = jnp.bfloat16, jnp.float32
    total, width = n1.shape
    ffn = upper.shape[1]
    small, mid, big = width // (2 * n_data), 3 * width // (2 * n_data), ffn // (2 * n_data)
    any_spec = pl.BlockSpec(memory_space=pl.ANY)
    vmem_spec = pl.BlockSpec(memory_space=pltpu.VMEM)
    out_shapes = [(loss_part.shape, f32), ((width, width), f32), ((3 * width, width), f32), ((ffn, width), f32), ((width, ffn), f32), (dx.shape, bf16)]
    n_spans = max(1, n_stages.bit_length() - 1)
    scratch = [
        pltpu.VMEM((total, width), bf16), pltpu.VMEM((total, width), bf16), pltpu.VMEM((total, width), bf16), pltpu.VMEM((total, width), bf16),
        pltpu.VMEM((2, small, total), bf16), pltpu.VMEM((2, mid, total), bf16),
        pltpu.VMEM((1, total, big), bf16), pltpu.VMEM((1, total, big), bf16),
        pltpu.VMEM((n_data, 2, small, width), f32), pltpu.VMEM((n_data, 2, mid, width), f32),
        pltpu.VMEM((n_data, 2, big, width), f32), pltpu.VMEM((n_data, 2, width, big), f32),
        pltpu.VMEM((n_data,) + loss_part.shape, f32),
        pltpu.SemaphoreType.DMA((4,)), pltpu.SemaphoreType.DMA((4, 2)),
        pltpu.SemaphoreType.DMA((n_data - 1, 4, 2)), pltpu.SemaphoreType.DMA((n_data - 1, 4, 2)),
        pltpu.SemaphoreType.DMA((n_data - 1, 4, 2)), pltpu.SemaphoreType.DMA((n_data - 1, 4, 2)),
        pltpu.SemaphoreType.DMA((4, 2)), pltpu.SemaphoreType.DMA((2, n_spans)),
        pltpu.SemaphoreType.DMA((n_data - 1,)), pltpu.SemaphoreType.DMA((n_data - 1,)), pltpu.SemaphoreType.DMA(()),
    ]
    flops = 2 * total * width * (4 * width + 2 * ffn)
    return pl.pallas_call(
        functools.partial(reduce_kernel, (n_data, n_stages)),
        out_shape=[jax.ShapeDtypeStruct(s, d) for s, d in out_shapes],
        in_specs=[any_spec] * 10,
        out_specs=[vmem_spec] + [any_spec] * 5,
        scratch_shapes=scratch,
        input_output_aliases={9: 5},
        compiler_params=pltpu.CompilerParams(collective_id=1, has_side_effects=True, vmem_limit_bytes=67043328),
        cost_estimate=pl.CostEstimate(flops=flops, bytes_accessed=150 * 2 ** 20, transcendentals=0),
        name='gradient_sums',
    )(loss_part, ctx_t, dhid, dqkv_t, n1, upper, grads, n2, dpre, dx)


def solution(mesh):
    n_stages = mesh.shape['stage']
    n_data = mesh.shape['data']
    act_spec = P(('rep', 'data'))
    weight_spec = P(('rep', 'stage'))

    def per_device(embeds, targets, w_qkv, w_out, w_up, w_down):
        n_micro, micro_b, seq_len, width = embeds.shape
        heads, hdim = w_qkv.shape[2], w_qkv.shape[3]
        grad_scale = 1.0 / (n_data * n_micro)
        loss_norm = 1.0 / (n_data * n_micro * micro_b * seq_len * width)
        flat = (n_micro * micro_b, seq_len, width)
        outs = run_pipeline(
            n_stages, grad_scale, embeds.reshape(flat), targets.reshape(flat), w_qkv.reshape(3 * width, width),
            w_out.reshape(width, width), w_up[0], w_down[0], heads, hdim)
        loss_part, n1, n2, upper, ctx_t, dqkv_t, dpre, dhid, grads, dx = outs[:10]
        loss_sum, d_out, d_qkv, d_down, d_up, d_embeds = sum_gradients(
            n_data, n_stages, loss_part, ctx_t, dhid, dqkv_t, n1, upper, grads, n2, dpre, dx)
        loss = (0.5 * loss_norm * jnp.sum(loss_sum)).reshape(1)
        return (loss, d_qkv.reshape(w_qkv.shape), d_out.reshape(w_out.shape), d_up[None], d_down[None], d_embeds.reshape(embeds.shape))

    return jax.shard_map(per_device, mesh=mesh, in_specs=(act_spec, act_spec, weight_spec, weight_spec, weight_spec, weight_spec), out_specs=(P('rep'), weight_spec, weight_spec, weight_spec, weight_spec, act_spec), check_vma=False)
```

time: 3750 us -> 892 us (0.24)
  waiting for transfers between devices: 1050 us -> 0 us
  Pallas kernels: 0 us -> 860 us
  other arithmetic: 838 us -> 1.29 us
  starting transfers between devices: 766 us -> 0 us
  matrix products: 521 us -> 0 us
  local copies, waits for them, and re-layouts: 368 us -> 23.5 us
  loops' own time: 141 us -> 0 us
  blocking collectives: 47.1 us -> 0 us
    pallas_call x0 -> x2, Pallas kernels: none -> 860 us  [the longest x1 467 us: sum_gradients(): pl.pallas_call(functools.partial(reduce_kernel, (n_data, n_stages)), out_...]
    ppermute x34 -> x0, starting transfers between devices: 766 us -> none  [the longest x17 552 us: tick_body(): from_prev = lax.ppermute(act_out, 'stage', next_pairs)]
    add x71 -> x0, other arithmetic: 640 us -> none  [the longest x68 637 us: tick_body(): total + piece]
    ppermute x34 -> x0, waiting for transfers between devices: 549 us -> none  [the longest x17 549 us: tick_body(): from_next = lax.ppermute(grad_in, 'stage', prev_pairs)]
    dot_general x63 -> x0, matrix products: 521 us -> none  [the longest x3 62 us: layer_backward(): jnp.einsum('bhqs,bhqk->bhsk', d_scores, query, preferred_element_type=jnp...]
    psum x2 -> x0, waiting for transfers between devices: 501 us -> none  [the longest x1 481 us: per_device(): d_weights = tuple((lax.psum(total, 'data')[None] for total in grad_sums))]
    another operation x102 -> x0, local copies, waits for them, and re-layouts: 248 us -> none
    another operation x35 -> x0, loops' own time: 141 us -> none  [the longest x17 67.6 us: tick_body(): lax.cond(bwd_valid, run_backward, skip_backward, (act_saved, grad_out))]
  transfers between devices with their start and end apart: 36 -> 0, of which waited for: 7 -> 0; matrix products, arithmetic and copies ran while one was open for 38% -> 0% of each run, Pallas kernels for 0% -> 0%
where the time goes in v1:
time: 892 us; the launch traced here: 887 us
  Pallas kernels  860 us (96%)
  local copies, waits for them, and re-layouts  23.5 us (3%)
    pallas_call x1, Pallas kernels, sum_gradients(): pl.pallas_call(functools.partial(reduce_kernel, (n_data, n_stages)), out_...  467 us
    pallas_call x1, Pallas kernels, run_pipeline(): pl.pallas_call(functools.partial(pipeline_kernel, (n_stages, n_seq, token...  392 us
    unnamed x19, local copies, waits for them, and re-layouts  23.5 us

profile of v1, /device:TPU:97, one launch (start us, length us, event | category | flops | bytes accessed | tf_op | source)
XLA Modules:
  0.0 887.0 jit_solution(16826902655466739497)
XLA Ops:
  0.6 392.5 %stage_pipeline.1 = (f32[8,128]{1,0:T(8,128)}, bf16[3072,768]{1,0:T(8,128)(2,1)}, bf16[3072,768]{1,0:T(8,128)(2,1)}, bf16[3072,3072]{1,0:T(8,128)(2,1)}, bf16[76...) custom-call(bf16[12,256,768]{2,1,0:T(8,128)(2,1)} %bitcast.21, ...), custom_call_target="tpu_custom_call" | custom-call | flops 130459631616 | bytes 209715200 | tf_op jit(solution)/shard_map/stage_pipeline/pallas_call | solution.py:430
  393.1 467.3 %gradient_sums.1 = (f32[8,128]{1,0:T(8,128)}, f32[768,768]{1,0:T(8,128)}, f32[2304,768]{1,0:T(8,128)}, f32[3072,768]{1,0:T(8,128)}, f32[768,3072]{1,0:T(8,128)}, /*index=5*/bf16[12,256,768]{2,1,0:T(8,128)(2,1)}) custom-call(f32[8,128]{1,0:T(8,128)} %get-tuple-element.22.loss_hbm, ...), custom_call_target="tpu_custom_call", output_to_operand_aliasing={{5}: (9, {})} | custom-call | flops 43486543872 | bytes 157286400 | tf_op jit(solution)/shard_map/gradient_sums/pallas_call | solution.py:684
  860.4 1.3 reduce_sum.9
  862.3 0.0 copy-start.1
  862.3 0.0 copy-start
  862.4 7.5 copy.19
  869.9 0.0 copy-done.1
  869.9 0.0 slice-start
  869.9 1.4 copy.20
  871.3 0.9 copy-done
  872.2 0.0 slice-start.1
  872.2 0.0 slice-start.2
  872.2 0.0 slice-start.3
  872.2 4.8 copy.21
  877.0 0.0 slice-done
  877.0 1.2 slice-done.1
  878.1 0.2 slice-done.2
  878.3 0.0 slice-start.4
  878.3 4.6 copy.22
  883.0 0.0 slice-done.3
  883.0 0.7 slice-done.4
  883.7 2.2 copy.23
  (2 shorter events, 0.0 us)
Async XLA Ops:
  862.3 7.5 copy-start.1
  862.3 9.8 %copy-start = (f32[768,3072]{1,0:T(8,128)S(1)}, f32[768,3072]{1,0:T(8,128)}, u32[]{:S(2)}) copy-start(f32[768,3072]{1,0:T(8,128)} %get-tuple-element.35) | copy-start | bytes 28311556
  869.9 7.1 slice-start
  872.2 6.0 slice-start.1
  872.2 6.2 slice-start.2
  872.2 10.8 %slice-start.3 = ((s8[4718592]{0:T(1024)(128)(4,1)}), s8[524288]{0:T(1024)(128)(4,1)S(1)}, s32[]{:S(2)}) async-start(s8[4718592]{0:T(1024)(128)(4,1)} %bitcast.17), calls=%async_computation.3 | async-start | bytes 1048576
  878.3 5.3 slice-start.4

commit v2 on v1

--- a/solution.py
+++ b/solution.py
@@ -161,6 +161,27 @@
     dact_ref[...] = dact.astype(jnp.bfloat16)
 
 
+class placement:
+    def __init__(self, n_stages):
+        row = lax.axis_index('data')
+        self.row = row
+        self.index = lax.axis_index('stage')
+        self.column = lax.div(self.index, 2)
+        self.core = lax.rem(self.index, 2)
+        self.upper = lax.div(row, 2)
+        self.half = lax.rem(self.upper + self.column, 2)
+        self.layer = 2 * self.column + self.half
+        self.home = self.layer
+        self.mate = 2 * self.column + 1 - self.core
+        across = 3 - row
+        along = lax.rem(self.index + jnp.where(self.half == 1, 2, n_stages - 2), n_stages)
+        self.mate_id = {'data': row, 'stage': self.mate}
+        self.across_id = {'data': across, 'stage': self.index}
+        self.along_id = {'data': row, 'stage': along}
+        self.next_id = {'data': jnp.where(self.half == 1, row, across), 'stage': jnp.where(self.half == 1, along, self.index)}
+        self.prev_id = {'data': jnp.where(self.half == 1, across, row), 'stage': jnp.where(self.half == 1, self.index, along)}
+
+
 def pipeline_kernel(
     cfg,
     emb_hbm, tgt_hbm, wqkv_hbm, wout_hbm, wup_hbm, wdown_hbm,
@@ -168,18 +189,27 @@
     wqkv, wout, wup, wdown, act, grad, out_s, dact_s,
     n1_s, n2_s, up_s, ctx_s, qkv_s, gp_s, hid_s, stat_s,
     dpre_s, dhid_s, dctx_s, dqkv_s,
-    w_sem, in_sem, act_sem, grad_sem, fout_sem, bin_sem, bout_sem, fsend_sem, bsend_sem, loss_acc, loss_sem,
+    w_sem, in_sem, act_sem, grad_sem, fout_sem, bin_sem, bout_sem, fsend_sem, bsend_sem, loss_acc, loss_sem, dx_sem,
 ):
     n_stages, n_seq, tokens, grad_scale, dims = cfg
-    stage = lax.axis_index('stage')
+    here = placement(n_stages)
+    stage, core, next_id, prev_id = here.layer, here.core, here.next_id, here.prev_id
     is_first = stage == 0
     is_last = stage == n_stages - 1
-    nxt = lax.rem(stage + 1, n_stages)
-    prv = lax.rem(stage + n_stages - 1, n_stages)
+    own_weights = here.layer == here.index
+    own_data = here.upper == core
+    feeds_first = (here.column == 0) & (here.half == 1) & (core == 1)
+    feeds_last = (here.column == n_stages // 2 - 1) & (here.half == 0) & (core == 1)
 
     weight_pairs = ((wqkv_hbm, wqkv), (wout_hbm, wout), (wup_hbm, wup), (wdown_hbm, wdown))
-    for idx, (src, dst) in enumerate(weight_pairs):
-        pltpu.make_async_copy(src, dst, w_sem.at[idx]).start()
+
+    def load_weight(idx):
+        return pltpu.make_async_copy(weight_pairs[idx][0], weight_pairs[idx][1], w_sem.at[idx])
+
+    def give_weight(idx):
+        return pltpu.make_async_remote_copy(
+            src_ref=weight_pairs[idx][0], dst_ref=weight_pairs[idx][1], send_sem=w_sem.at[4 + idx], recv_sem=w_sem.at[8 + idx],
+            device_id=here.mate_id, device_id_type=MESH_ID)
 
     def load_embed(m):
         return pltpu.make_async_copy(emb_hbm.at[m], act.at[m], in_sem.at[m])
@@ -187,41 +217,73 @@
     def load_target(m):
         return pltpu.make_async_copy(tgt_hbm.at[m], grad.at[m], in_sem.at[m])
 
-    @pl.when(is_first)
+    def give_embed(m):
+        return pltpu.make_async_remote_copy(
+            src_ref=emb_hbm.at[m], dst_ref=act.at[m], send_sem=in_sem.at[m], recv_sem=act_sem.at[m],
+            device_id=here.across_id, device_id_type=MESH_ID)
+
+    def give_target(m):
+        return pltpu.make_async_remote_copy(
+            src_ref=tgt_hbm.at[m], dst_ref=grad.at[m], send_sem=in_sem.at[m], recv_sem=grad_sem.at[m],
+            device_id=here.across_id, device_id_type=MESH_ID)
+
+    def each_seq(when, action):
+        @pl.when(when)
+        def _():
+            def go(m, carry):
+                action(m)
+                return carry
+            lax.fori_loop(0, n_seq, go, 0)
+
+    @pl.when(own_weights)
     def _():
-        def go(m, carry):
-            load_embed(m).start()
-            return carry
-        lax.fori_loop(0, n_seq, go, 0)
-
-    @pl.when(is_last)
+        for idx in range(4):
+            load_weight(idx).start()
+
+    each_seq(is_first & own_data, lambda m: load_embed(m).start())
+    each_seq(is_last & own_data, lambda m: load_target(m).start())
+
+    barrier = pltpu.get_barrier_semaphore()
+    for peer in (here.mate_id, here.across_id, here.along_id):
+        pl.semaphore_signal(barrier, inc=1, device_id=peer, device_id_type=MESH_ID)
+    pl.semaphore_wait(barrier, 3)
+
+    @pl.when(own_weights)
     def _():
-        def go(m, carry):
-            load_target(m).start()
-            return carry
-        lax.fori_loop(0, n_seq, go, 0)
-
-    barrier = pltpu.get_barrier_semaphore()
-    for peer in (prv, nxt):
-        pl.semaphore_signal(barrier, inc=1, device_id={'stage': peer}, device_id_type=MESH_ID)
-    pl.semaphore_wait(barrier, 2)
-
+        for idx in range(4):
+            give_weight(idx).start()
+
+    each_seq(feeds_first, lambda m: give_embed(m).start())
+    each_seq(feeds_last, lambda m: give_target(m).start())
     loss_acc[...] = jnp.zeros_like(loss_acc)
-    for idx, (src, dst) in enumerate(weight_pairs):
-        pltpu.make_async_copy(src, dst, w_sem.at[idx]).wait()
+
+    @pl.when(own_weights)
+    def _():
+        for idx in range(4):
+            load_weight(idx).wait()
+
+    @pl.when(jnp.logical_not(own_weights))
+    def _():
+        for idx in range(4):
+            give_weight(idx).wait_recv()
 
     def send_act(m, slot):
         return pltpu.make_async_remote_copy(
             src_ref=out_s.at[slot], dst_ref=act.at[m], send_sem=fsend_sem.at[slot], recv_sem=act_sem.at[m],
-            device_id={'stage': nxt}, device_id_type=MESH_ID)
+            device_id=next_id, device_id_type=MESH_ID)
 
     def send_grad(m, slot):
         return pltpu.make_async_remote_copy(
             src_ref=dact_s.at[slot], dst_ref=grad.at[m], send_sem=bsend_sem.at[slot], recv_sem=grad_sem.at[m],
-            device_id={'stage': prv}, device_id_type=MESH_ID)
+            device_id=prev_id, device_id_type=MESH_ID)
 
     def store_dx(m, slot):
         return pltpu.make_async_copy(dact_s.at[slot], dx_hbm.at[m], bsend_sem.at[slot])
+
+    def give_dx(m, slot):
+        return pltpu.make_async_remote_copy(
+            src_ref=dact_s.at[slot], dst_ref=dx_hbm.at[m], send_sem=bsend_sem.at[slot], recv_sem=dx_sem.at[m],
+            device_id=here.across_id, device_id_type=MESH_ID)
 
     def token_range(m):
         return pl.ds(pl.multiple_of(m * tokens, tokens), tokens)
@@ -275,11 +337,11 @@
             m = fwd_m
             slot = lax.rem(m, 2)
 
-            @pl.when(is_first)
+            @pl.when(is_first & own_data)
             def _():
                 load_embed(m).wait()
 
-            @pl.when(jnp.logical_not(is_first))
+            @pl.when(jnp.logical_not(is_first & own_data))
             def _():
                 send_act(m, slot).wait_recv()
 
@@ -292,9 +354,16 @@
             def _():
                 send_act(m, slot).start()
 
+            @pl.when(is_last & own_data)
+            def _():
+                load_target(m).wait()
+
+            @pl.when(is_last & jnp.logical_not(own_data))
+            def _():
+                send_grad(m, slot).wait_recv()
+
             @pl.when(is_last)
             def _():
-                load_target(m).wait()
                 error = out_s[slot].astype(jnp.float32) - grad[m].astype(jnp.float32)
                 square = error * error
                 total = square[0:8]
@@ -324,9 +393,13 @@
             def _():
                 send_grad(m, slot).start()
 
-            @pl.when(is_first)
+            @pl.when(is_first & own_data)
             def _():
                 store_dx(m, slot).start()
+
+            @pl.when(is_first & jnp.logical_not(own_data))
+            def _():
+                give_dx(m, slot).start()
 
         fwd_old = fwd_m - 1
         bwd_old = bwd_m - 1
@@ -351,9 +424,13 @@
             def _():
                 send_grad(bwd_old, slot).wait_send()
 
-            @pl.when(is_first)
+            @pl.when(is_first & own_data)
             def _():
                 store_dx(bwd_old, slot).wait()
+
+            @pl.when(is_first & jnp.logical_not(own_data))
+            def _():
+                give_dx(bwd_old, slot).wait_send()
 
         @pl.when(in_range(bwd_m + 1) & jnp.logical_not(is_last))
         def _():
@@ -367,7 +444,7 @@
     def send_loss():
         return pltpu.make_async_remote_copy(
             src_ref=loss_ref, dst_ref=loss_ref, send_sem=loss_sem.at[0], recv_sem=loss_sem.at[1],
-            device_id={'stage': prv}, device_id_type=MESH_ID)
+            device_id=prev_id, device_id_type=MESH_ID)
 
     @pl.when(is_last)
     def _():
@@ -385,6 +462,15 @@
     def _():
         send_loss().start()
         send_loss().wait_send()
+
+    @pl.when(own_weights)
+    def _():
+        for idx in range(4):
+            give_weight(idx).wait_send()
+
+    each_seq(feeds_first, lambda m: give_embed(m).wait_send())
+    each_seq(feeds_last, lambda m: give_target(m).wait_send())
+    each_seq(feeds_first, lambda m: give_dx(m, 0).wait_recv())
 
 
 def run_pipeline(n_stages, grad_scale, embeds, targets, wqkv, wout, wup, wdown, heads, hdim):
@@ -420,11 +506,11 @@
         pltpu.VMEM((3, tokens, width), bf16), pltpu.VMEM((3, heads, 8, tokens), f32),
         pltpu.VMEM((2, tokens, ffn), bf16), pltpu.VMEM((2, tokens, width), bf16),
         pltpu.VMEM((width, tokens), bf16), pltpu.VMEM((2, 3 * width, tokens), bf16),
-        pltpu.SemaphoreType.DMA((4,)), pltpu.SemaphoreType.DMA((n_seq,)),
+        pltpu.SemaphoreType.DMA((12,)), pltpu.SemaphoreType.DMA((n_seq,)),
         pltpu.SemaphoreType.DMA((n_seq,)), pltpu.SemaphoreType.DMA((n_seq,)),
         pltpu.SemaphoreType.DMA((2, 8)), pltpu.SemaphoreType.DMA((4,)), pltpu.SemaphoreType.DMA((2, 4)),
         pltpu.SemaphoreType.DMA((2,)), pltpu.SemaphoreType.DMA((2,)),
-        pltpu.VMEM((8, width), f32), pltpu.SemaphoreType.DMA((2,)),
+        pltpu.VMEM((8, width), f32), pltpu.SemaphoreType.DMA((2,)), pltpu.SemaphoreType.DMA((n_seq,)),
     ]
     linear = 2 * total * (wqkv.size + wout.size + wup.size + wdown.size)
     return pl.pallas_call(
@@ -443,117 +529,136 @@
     cfg,
     loss_hbm, ctx_hbm, dhid_hbm, dqkv_hbm, n1_hbm, up_hbm, g_hbm, n2_hbm, dpre_hbm, dx_hbm,
     loss_ref, dout_hbm, dqkvw_hbm, ddown_hbm, dup_hbm, demb_hbm,
-    out_res, qkv_res, down_res, up_res, out_in, qkv_in, down_in, up_in, out_sl, qkv_sl, down_sl, up_sl, loss_sl,
-    res_sem, in_sem, rs_send, rs_recv, ag_send, ag_recv, store_sem, dx_sem, loss_send, loss_recv, loss_in,
+    out_res, qkv_res, down_res, up_res, out_in, qkv_in, down_in, up_in,
+    out_give, qkv_give, down_give, up_give, out_core, qkv_core, down_core, up_core, out_row, qkv_row, down_row, up_row, loss_sl,
+    res_sem, in_sem, give_sem, core_sem, row_send, row_recv, put_send, put_recv, pass_send, store_sem, dx_sem,
+    loss_send, loss_recv, loss_in,
 ):
-    n_data, n_stages = cfg
-    rank = lax.axis_index('data')
-    stage = lax.axis_index('stage')
-    right = lax.rem(rank + 1, n_data)
-    left = lax.rem(rank + n_data - 1, n_data)
-    toward = (right, left)
-    last = n_data - 1
+    (n_stages,) = cfg
+    here = placement(n_stages)
+    row, core, stage = here.row, here.core, here.index
+    pair = lax.rem(row, 2)
+    pair_row = row + 1 - 2 * pair
+    across = 3 - row
+    is_home = here.home == stage
+    home_id = {'data': row, 'stage': here.home}
+    pair_id = {'data': pair_row, 'stage': stage}
+    pair_home_id = {'data': pair_row, 'stage': here.home}
+    across_home_id = {'data': across, 'stage': here.home}
 
     kinds = (
-        ('rows', dhid_hbm, out_res, ctx_hbm, out_in, out_sl, dout_hbm),
-        ('rows', n1_hbm, qkv_res, dqkv_hbm, qkv_in, qkv_sl, dqkvw_hbm),
-        ('tall', g_hbm, down_res, up_hbm, down_in, down_sl, ddown_hbm),
-        ('wide', n2_hbm, up_res, dpre_hbm, up_in, up_sl, dup_hbm),
+        ('rows', dhid_hbm, out_res, ctx_hbm, out_in, out_give, out_core, out_row, dout_hbm),
+        ('rows', n1_hbm, qkv_res, dqkv_hbm, qkv_in, qkv_give, qkv_core, qkv_row, dqkvw_hbm),
+        ('tall', g_hbm, down_res, up_hbm, down_in, down_give, down_core, down_row, ddown_hbm),
+        ('wide', n2_hbm, up_res, dpre_hbm, up_in, up_give, up_core, up_row, dup_hbm),
     )
-    order = ((0, 0), (0, 1), (1, 0), (1, 1), (2, 0), (3, 0), (2, 1), (3, 1))
-
-    def owner_of(step, way):
-        turn = step + 1
-        return lax.rem(rank + (n_data - turn if way == 0 else turn), n_data)
-
-    def piece(kind, way, owner):
+    n_kinds = len(kinds)
+    turns = ((1, 1), (0, 1), (1, 0), (0, 0))
+
+    def piece(kind, member, unit, num):
         size = kinds[kind][4].shape[1 if kinds[kind][0] == 'rows' else 2]
-        return pl.ds(pl.multiple_of((way * n_data + owner) * size, size), size)
-
-    def read_piece(kind, way, step):
-        form, _, _, src, buf, _, _ = kinds[kind]
-        part = piece(kind, way, owner_of(step, way))
+        return pl.ds(pl.multiple_of(((member * 2 + unit) * 2 + num) * size, size), size)
+
+    def flip(val, by):
+        return 1 - val if by else val
+
+    def read_piece(kind, turn, num):
+        form, _, _, src, buf = kinds[kind][:5]
+        part = piece(kind, flip(pair, turns[turn][0]), flip(core, turns[turn][1]), num)
         view = src.at[part, :] if form == 'rows' else src.at[:, part]
-        buf_idx = way if buf.shape[0] == 2 else 0
-        return pltpu.make_async_copy(view, buf.at[buf_idx], in_sem.at[kind, buf_idx])
-
-    def out_view(kind, way, owner):
-        part = piece(kind, way, owner)
-        dst = kinds[kind][6]
+        return pltpu.make_async_copy(view, buf.at[turn % 2], in_sem.at[kind, turn % 2])
+
+    def out_view(kind, member, unit, num):
+        part = piece(kind, member, unit, num)
+        dst = kinds[kind][8]
         return dst.at[:, part] if kinds[kind][0] == 'wide' else dst.at[part, :]
 
-    def pass_sum(kind, way, step):
-        slots = kinds[kind][5]
-        return pltpu.make_async_remote_copy(
-            src_ref=slots.at[step, way], dst_ref=slots.at[step + 1, way], send_sem=rs_send.at[step, kind, way],
-            recv_sem=rs_recv.at[step, kind, way], device_id={'data': toward[way]}, device_id_type=MESH_ID)
-
-    def share(kind, way, step):
-        owner = lax.rem(rank + (n_data - step if way == 0 else step), n_data)
-        view = out_view(kind, way, owner)
-        return pltpu.make_async_remote_copy(
-            src_ref=kinds[kind][5].at[last, way] if step == 0 else view, dst_ref=view,
-            send_sem=ag_send.at[step, kind, way], recv_sem=ag_recv.at[step, kind, way],
-            device_id={'data': toward[way]}, device_id_type=MESH_ID)
-
-    def shared_in(kind, way, step):
-        owner = lax.rem(rank + (n_data - step - 1 if way == 0 else step + 1), n_data)
-        view = out_view(kind, way, owner)
-        return pltpu.make_async_remote_copy(
-            src_ref=view, dst_ref=view, send_sem=ag_send.at[step, kind, way], recv_sem=ag_recv.at[step, kind, way],
-            device_id={'data': toward[way]}, device_id_type=MESH_ID)
-
-    def keep(kind, way):
-        return pltpu.make_async_copy(kinds[kind][5].at[last, way], out_view(kind, way, rank), store_sem.at[kind, way])
+    def give(kind, other, num):
+        return pltpu.make_async_remote_copy(
+            src_ref=kinds[kind][5].at[other], dst_ref=kinds[kind][6].at[num, other], send_sem=give_sem.at[kind, other],
+            recv_sem=core_sem.at[kind, num, other], device_id=here.mate_id, device_id_type=MESH_ID)
+
+    def send_row(kind, num):
+        return pltpu.make_async_remote_copy(
+            src_ref=kinds[kind][6].at[num, 1], dst_ref=kinds[kind][7].at[num], send_sem=row_send.at[kind, num],
+            recv_sem=row_recv.at[kind, num], device_id=pair_id, device_id_type=MESH_ID)
+
+    def put(kind, num, target, device_id):
+        return pltpu.make_async_remote_copy(
+            src_ref=kinds[kind][7].at[num], dst_ref=out_view(kind, pair, core, num), send_sem=put_send.at[target, kind, num],
+            recv_sem=put_recv.at[pair, core, kind, num], device_id=device_id, device_id_type=MESH_ID)
+
+    def keep(kind, num):
+        return pltpu.make_async_copy(kinds[kind][7].at[num], out_view(kind, pair, core, num), store_sem.at[kind, num])
+
+    def arrival(kind, num, member, unit):
+        view = out_view(kind, member, unit, num)
+        return pltpu.make_async_remote_copy(
+            src_ref=view, dst_ref=view, send_sem=pass_send.at[unit, kind, num], recv_sem=put_recv.at[member, unit, kind, num],
+            device_id=across_home_id, device_id_type=MESH_ID)
 
     def load_resident(kind):
         return pltpu.make_async_copy(kinds[kind][1], kinds[kind][2], res_sem.at[kind])
 
-    my_loss = pltpu.make_async_copy(loss_hbm, loss_sl.at[rank], loss_in)
+    def pipeline_id(row_idx, unit):
+        return 2 * jnp.minimum(row_idx, 3 - row_idx) + unit
+
+    my_loss = pltpu.make_async_copy(loss_hbm, loss_sl.at[pipeline_id(row, core)], loss_in)
     my_loss.start()
-    for kind in range(len(kinds)):
+    for kind in range(n_kinds):
         load_resident(kind).start()
-        for way in range(kinds[kind][4].shape[0]):
-            read_piece(kind, way, 0).start()
-
+        read_piece(kind, 0, 0).start()
+
+    source = here.upper
+    rank = stage + source - 2 * source * core
     spans = []
     span = n_stages // 2
     while span >= 1:
         spans.append(span)
         span //= 2
+
+    def swapped(span):
+        return stage + span - 2 * span * lax.rem(lax.div(stage, span), 2)
+
+    loss_ids = (
+        ({'data': row, 'stage': here.mate}, row, 1 - core),
+        ({'data': pair_row, 'stage': stage}, pair_row, core),
+        ({'data': pair_row, 'stage': here.mate}, pair_row, 1 - core),
+    )
+    peers = [ident for ident, _, _ in loss_ids]
+    peers += [{'data': across, 'stage': stage}, {'data': across, 'stage': here.mate}]
+    peers += [{'data': row, 'stage': swapped(span)} for span in spans if span > 1]
     barrier = pltpu.get_barrier_semaphore()
-    for turn in range(1, n_data):
-        pl.semaphore_signal(barrier, inc=1, device_id={'data': lax.rem(rank + turn, n_data)}, device_id_type=MESH_ID)
-    for span in spans:
-        upper = lax.rem(lax.div(stage, span), 2)
-        pl.semaphore_signal(barrier, inc=1, device_id={'stage': stage + span - 2 * span * upper}, device_id_type=MESH_ID)
-    pl.semaphore_wait(barrier, n_data - 1 + len(spans))
-
-    def send_loss(turn):
-        return pltpu.make_async_remote_copy(
-            src_ref=loss_sl.at[rank], dst_ref=loss_sl.at[rank], send_sem=loss_send.at[turn - 1], recv_sem=loss_recv.at[turn - 1],
-            device_id={'data': lax.rem(rank + turn, n_data)}, device_id_type=MESH_ID)
-
-    def loss_arrival(turn):
-        sender = lax.rem(rank + n_data - turn, n_data)
-        return pltpu.make_async_remote_copy(
-            src_ref=loss_sl.at[sender], dst_ref=loss_sl.at[sender], send_sem=loss_send.at[turn - 1], recv_sem=loss_recv.at[turn - 1],
-            device_id={'data': lax.rem(rank + turn, n_data)}, device_id_type=MESH_ID)
+    for ident in peers:
+        pl.semaphore_signal(barrier, inc=1, device_id=ident, device_id_type=MESH_ID)
+    pl.semaphore_wait(barrier, len(peers))
+
+    def send_loss(idx):
+        slot = loss_sl.at[pipeline_id(row, core)]
+        return pltpu.make_async_remote_copy(
+            src_ref=slot, dst_ref=slot, send_sem=loss_send.at[idx], recv_sem=loss_recv.at[idx],
+            device_id=loss_ids[idx][0], device_id_type=MESH_ID)
+
+    def loss_arrival(idx):
+        slot = loss_sl.at[pipeline_id(loss_ids[idx][1], loss_ids[idx][2])]
+        return pltpu.make_async_remote_copy(
+            src_ref=slot, dst_ref=slot, send_sem=loss_send.at[idx], recv_sem=loss_recv.at[idx],
+            device_id=loss_ids[idx][0], device_id_type=MESH_ID)
 
     my_loss.wait()
-    for turn in range(1, n_data):
-        send_loss(turn).start()
+    for idx in range(3):
+        send_loss(idx).start()
 
     def spread(idx):
         return pltpu.make_async_remote_copy(
             src_ref=demb_hbm, dst_ref=demb_hbm, send_sem=dx_sem.at[0, idx], recv_sem=dx_sem.at[1, idx],
-            device_id={'stage': lax.rem(stage + spans[idx], n_stages)}, device_id_type=MESH_ID)
+            device_id={'data': row, 'stage': swapped(spans[idx])}, device_id_type=MESH_ID)
 
     def sends_at(idx):
-        return lax.rem(stage, 2 * spans[idx]) == 0
+        return lax.rem(rank, 2 * spans[idx]) == 0
 
     def receives_at(idx):
-        return lax.rem(stage, 2 * spans[idx]) == spans[idx]
+        return lax.rem(rank, 2 * spans[idx]) == spans[idx]
 
     def spread_round(idx):
         if idx > 0:
@@ -565,124 +670,165 @@
             def _():
                 spread(idx).start()
 
-    for kind in range(len(kinds)):
-        slots = kinds[kind][5]
-        for way in range(2):
-            slots[0, way] = jnp.zeros(slots.shape[2:], slots.dtype)
-
-    def add_product(kind, way, step):
-        form, _, res, _, buf, slots, _ = kinds[kind]
-        fed = buf.at[way if buf.shape[0] == 2 else 0]
+    def product(kind, turn, num, sink, base):
+        form, _, res, _, buf = kinds[kind][:5]
+        read_piece(kind, turn, num).wait()
+        if turn < 3:
+            read_piece(kind, turn + 1, num).start()
+        else:
+            @pl.when(num == 0)
+            def _():
+                read_piece(kind, 0, 1).start()
+        fed = buf.at[turn % 2]
         tile = min(256, res.shape[1])
 
         def body(n, carry):
-            cols = pl.ds(pl.multiple_of(n * tile, tile), tile)
+            span = pl.ds(pl.multiple_of(n * tile, tile), tile)
             if form == 'rows':
-                slots[step, way, :, cols] += dot_nn(fed[...], res[:, cols])
+                part, at = dot_nn(fed[...], res[:, span]), (slice(None), span)
             elif form == 'tall':
-                slots[step, way, :, cols] += dot_tn(fed[...], res[:, cols])
+                part, at = dot_tn(fed[...], res[:, span]), (slice(None), span)
             else:
-                slots[step, way, cols, :] += dot_tn(res[:, cols], fed[...])
+                part, at = dot_tn(res[:, span], fed[...]), (span, slice(None))
+            for ref in base:
+                part = part + ref[at]
+            sink[at] = part
             return carry
 
         lax.fori_loop(0, res.shape[1] // tile, body, 0)
 
-    def ring_step(step, carry):
-        for kind, way in order:
-            @pl.when(step == 0)
-            def _():
-                if way == 0:
-                    load_resident(kind).wait()
-
-            read_piece(kind, way, step).wait()
-
-            @pl.when(step > 0)
-            def _():
-                pass_sum(kind, way, step - 1).wait_recv()
-
-            add_product(kind, way, step)
-            if kinds[kind][4].shape[0] == 2:
-                @pl.when(step < last)
+    def first_half(kind, num):
+        give_buf, core_buf = kinds[kind][5:7]
+
+        @pl.when(num == 0)
+        def _():
+            load_resident(kind).wait()
+
+        for turn, other in ((0, 1), (1, 0)):
+            @pl.when(num > 0)
+            def _():
+                give(kind, other, num - 1).wait_send()
+
+            product(kind, turn, num, give_buf.at[other], ())
+            give(kind, other, num).start()
+        give(kind, 1, num).wait_recv()
+        product(kind, 2, num, core_buf.at[num, 1], (core_buf.at[num, 1],))
+        send_row(kind, num).start()
+
+    def second_half(kind, num):
+        core_buf, row_buf = kinds[kind][6:8]
+        give(kind, 0, num).wait_recv()
+        send_row(kind, num).wait_recv()
+        product(kind, 3, num, row_buf.at[num], (core_buf.at[num, 0], row_buf.at[num]))
+        put(kind, num, 1, pair_home_id).start()
+        put(kind, num, 2, across_home_id).start()
+
+        @pl.when(is_home)
+        def _():
+            keep(kind, num).start()
+
+        @pl.when(jnp.logical_not(is_home))
+        def _():
+            put(kind, num, 0, home_id).start()
+
+    def pass_on(kind, num):
+        @pl.when(is_home)
+        def _():
+            for unit in range(2):
+                arrival(kind, num, 1 - pair, unit).wait_recv()
+                arrival(kind, num, 1 - pair, unit).start()
+
+    def round_body(num, carry):
+        for kind in range(n_kinds):
+            first_half(kind, num)
+            if kind >= 1:
+                second_half(kind - 1, num)
+            else:
+                @pl.when(num > 0)
                 def _():
-                    read_piece(kind, way, step + 1).start()
-            elif way == 0:
-                read_piece(kind, 1, step).start()
+                    second_half(n_kinds - 1, num - 1)
+            if kind >= 2:
+                pass_on(kind - 2, num)
             else:
-                @pl.when(step < last)
+                @pl.when(num > 0)
                 def _():
-                    read_piece(kind, 0, step + 1).start()
-
-            @pl.when(step < last)
-            def _():
-                pass_sum(kind, way, step).start()
-
-            @pl.when(step == last)
-            def _():
-                keep(kind, way).start()
-                share(kind, way, 0).start()
-
-        for idx in range(min(last, len(spans))):
-            @pl.when(step == idx)
-            def _():
-                spread_round(idx)
+                    pass_on(kind + 2, num - 1)
+        for idx in range(2):
+            if idx < len(spans):
+                @pl.when(num == idx)
+                def _():
+                    spread_round(idx)
         return carry
 
-    lax.fori_loop(0, n_data, ring_step, 0)
-
-    for idx in range(min(last, len(spans)), len(spans) + 1):
+    lax.fori_loop(0, 2, round_body, 0)
+    second_half(n_kinds - 1, 1)
+    for idx in range(min(2, len(spans)), len(spans) + 1):
         spread_round(idx)
-    for step in range(1, last):
-        for kind, way in order:
-            shared_in(kind, way, step - 1).wait_recv()
-            share(kind, way, step).start()
-
-    for turn in range(1, n_data):
-        loss_arrival(turn).wait_recv()
+    pass_on(n_kinds - 2, 1)
+    pass_on(n_kinds - 1, 1)
+
+    for idx in range(3):
+        loss_arrival(idx).wait_recv()
     total = loss_sl[0]
-    for idx in range(1, n_data):
+    for idx in range(1, 4):
         total = total + loss_sl[idx]
     loss_ref[...] = total
 
-    for kind, way in order:
-        shared_in(kind, way, last - 1).wait_recv()
-    for kind, way in order:
-        keep(kind, way).wait()
-        for step in range(last):
-            pass_sum(kind, way, step).wait_send()
-            share(kind, way, step).wait_send()
-    for turn in range(1, n_data):
-        send_loss(turn).wait_send()
+    for kind in range(n_kinds):
+        for num in range(2):
+            @pl.when(is_home)
+            def _():
+                arrival(kind, num, pair, 1 - core).wait_recv()
+                keep(kind, num).wait()
+                for unit in range(2):
+                    arrival(kind, num, 1 - pair, unit).wait_send()
+
+            @pl.when(jnp.logical_not(is_home))
+            def _():
+                for member in range(2):
+                    for unit in range(2):
+                        arrival(kind, num, member, unit).wait_recv()
+                put(kind, num, 0, home_id).wait_send()
+
+            send_row(kind, num).wait_send()
+            put(kind, num, 1, pair_home_id).wait_send()
+            put(kind, num, 2, across_home_id).wait_send()
+        for other in range(2):
+            give(kind, other, 1).wait_send()
+    for idx in range(3):
+        send_loss(idx).wait_send()
     for idx in range(len(spans)):
         @pl.when(sends_at(idx))
         def _():
             spread(idx).wait_send()
 
 
-def sum_gradients(n_data, n_stages, loss_part, ctx_t, dhid, dqkv_t, n1, upper, grads, n2, dpre, dx):
+def sum_gradients(n_stages, loss_part, ctx_t, dhid, dqkv_t, n1, upper, grads, n2, dpre, dx):
     bf16, f32 = jnp.bfloat16, jnp.float32
     total, width = n1.shape
     ffn = upper.shape[1]
-    small, mid, big = width // (2 * n_data), 3 * width // (2 * n_data), ffn // (2 * n_data)
+    small, mid, big = width // 8, 3 * width // 8, ffn // 8
     any_spec = pl.BlockSpec(memory_space=pl.ANY)
     vmem_spec = pl.BlockSpec(memory_space=pltpu.VMEM)
     out_shapes = [(loss_part.shape, f32), ((width, width), f32), ((3 * width, width), f32), ((ffn, width), f32), ((width, ffn), f32), (dx.shape, bf16)]
-    n_spans = max(1, n_stages.bit_length() - 1)
-    scratch = [
-        pltpu.VMEM((total, width), bf16), pltpu.VMEM((total, width), bf16), pltpu.VMEM((total, width), bf16), pltpu.VMEM((total, width), bf16),
+    n_spans = n_stages.bit_length() - 1
+    pieces = ((small, width), (mid, width), (big, width), (width, big))
+    dma = pltpu.SemaphoreType.DMA
+    scratch = [pltpu.VMEM((total, width), bf16)] * 4 + [
         pltpu.VMEM((2, small, total), bf16), pltpu.VMEM((2, mid, total), bf16),
-        pltpu.VMEM((1, total, big), bf16), pltpu.VMEM((1, total, big), bf16),
-        pltpu.VMEM((n_data, 2, small, width), f32), pltpu.VMEM((n_data, 2, mid, width), f32),
-        pltpu.VMEM((n_data, 2, big, width), f32), pltpu.VMEM((n_data, 2, width, big), f32),
-        pltpu.VMEM((n_data,) + loss_part.shape, f32),
-        pltpu.SemaphoreType.DMA((4,)), pltpu.SemaphoreType.DMA((4, 2)),
-        pltpu.SemaphoreType.DMA((n_data - 1, 4, 2)), pltpu.SemaphoreType.DMA((n_data - 1, 4, 2)),
-        pltpu.SemaphoreType.DMA((n_data - 1, 4, 2)), pltpu.SemaphoreType.DMA((n_data - 1, 4, 2)),
-        pltpu.SemaphoreType.DMA((4, 2)), pltpu.SemaphoreType.DMA((2, n_spans)),
-        pltpu.SemaphoreType.DMA((n_data - 1,)), pltpu.SemaphoreType.DMA((n_data - 1,)), pltpu.SemaphoreType.DMA(()),
+        pltpu.VMEM((2, total, big), bf16), pltpu.VMEM((2, total, big), bf16),
+    ]
+    scratch += [pltpu.VMEM((2,) + p, f32) for p in pieces]
+    scratch += [pltpu.VMEM((2, 2) + p, f32) for p in pieces]
+    scratch += [pltpu.VMEM((2,) + p, f32) for p in pieces]
+    scratch += [
+        pltpu.VMEM((4,) + loss_part.shape, f32),
+        dma((4,)), dma((4, 2)), dma((4, 2)), dma((4, 2, 2)), dma((4, 2)), dma((4, 2)), dma((3, 4, 2)), dma((2, 2, 4, 2)),
+        dma((2, 4, 2)), dma((4, 2)), dma((2, n_spans)), dma((3,)), dma((3,)), dma(()),
     ]
     flops = 2 * total * width * (4 * width + 2 * ffn)
     return pl.pallas_call(
-        functools.partial(reduce_kernel, (n_data, n_stages)),
+        functools.partial(reduce_kernel, (n_stages,)),
         out_shape=[jax.ShapeDtypeStruct(s, d) for s, d in out_shapes],
         in_specs=[any_spec] * 10,
         out_specs=[vmem_spec] + [any_spec] * 5,
@@ -711,7 +857,7 @@
             w_out.reshape(width, width), w_up[0], w_down[0], heads, hdim)
         loss_part, n1, n2, upper, ctx_t, dqkv_t, dpre, dhid, grads, dx = outs[:10]
         loss_sum, d_out, d_qkv, d_down, d_up, d_embeds = sum_gradients(
-            n_data, n_stages, loss_part, ctx_t, dhid, dqkv_t, n1, upper, grads, n2, dpre, dx)
+            n_stages, loss_part, ctx_t, dhid, dqkv_t, n1, upper, grads, n2, dpre, dx)
         loss = (0.5 * loss_norm * jnp.sum(loss_sum)).reshape(1)
         return (loss, d_qkv.reshape(w_qkv.shape), d_out.reshape(w_out.shape), d_up[None], d_down[None], d_embeds.reshape(embeds.shape))
 

time: 892 us -> 867 us (0.972)
  Pallas kernels: 860 us -> 830 us
    pallas_call x1, Pallas kernels: 467 us -> 346 us  [sum_gradients(): pl.pallas_call(functools.partial(reduce_kernel, (n_stages,)), out_shape=[...]
    pallas_call x1, Pallas kernels: 392 us -> 484 us  [run_pipeline(): pl.pallas_call(functools.partial(pipeline_kernel, (n_stages, n_seq, token...]
where the time goes in v2:
time: 867 us; the launch traced here: 857 us
  Pallas kernels  830 us (96%)
  local copies, waits for them, and re-layouts  23.5 us (3%)
    pallas_call x1, Pallas kernels, run_pipeline(): pl.pallas_call(functools.partial(pipeline_kernel, (n_stages, n_seq, token...  484 us
    pallas_call x1, Pallas kernels, sum_gradients(): pl.pallas_call(functools.partial(reduce_kernel, (n_stages,)), out_shape=[...  346 us
    unnamed x19, local copies, waits for them, and re-layouts  23.5 us

profile of v2, /device:TPU:97, one launch (start us, length us, event | category | flops | bytes accessed | tf_op | source)
XLA Modules:
  0.0 856.8 jit_solution(12806109892033088881)
XLA Ops:
  0.6 484.1 %stage_pipeline.1 = (f32[8,128]{1,0:T(8,128)}, bf16[3072,768]{1,0:T(8,128)(2,1)}, bf16[3072,768]{1,0:T(8,128)(2,1)}, bf16[3072,3072]{1,0:T(8,128)(2,1)}, bf16[76...) custom-call(bf16[12,256,768]{2,1,0:T(8,128)(2,1)} %bitcast.21, ...), custom_call_target="tpu_custom_call" | custom-call | flops 130459631616 | bytes 209715200 | tf_op jit(solution)/shard_map/stage_pipeline/pallas_call | solution.py:516
  484.7 345.5 %gradient_sums.1 = (f32[8,128]{1,0:T(8,128)}, f32[768,768]{1,0:T(8,128)}, f32[2304,768]{1,0:T(8,128)}, f32[3072,768]{1,0:T(8,128)}, f32[768,3072]{1,0:T(8,128)}, /*index=5*/bf16[12,256,768]{2,1,0:T(8,128)(2,1)}) custom-call(f32[8,128]{1,0:T(8,128)} %get-tuple-element.22.loss_hbm, ...), custom_call_target="tpu_custom_call", output_to_operand_aliasing={{5}: (9, {})} | custom-call | flops 43486543872 | bytes 157286400 | tf_op jit(solution)/shard_map/gradient_sums/pallas_call | solution.py:830
  830.3 1.3 reduce_sum.9
  832.2 0.0 copy-start.1
  832.2 0.0 copy-start
  832.2 7.5 copy.19
  839.7 0.0 copy-done.1
  839.7 0.0 slice-start
  839.7 1.4 copy.20
  841.1 0.9 copy-done
  842.0 0.0 slice-start.1
  842.0 0.0 slice-start.2
  842.0 0.0 slice-start.3
  842.0 4.8 copy.21
  846.8 0.0 slice-done
  846.8 1.2 slice-done.1
  848.0 0.2 slice-done.2
  848.2 0.0 slice-start.4
  848.2 4.6 copy.22
  852.9 0.0 slice-done.3
  852.9 0.7 slice-done.4
  853.5 2.2 copy.23
  (2 shorter events, 0.0 us)
Async XLA Ops:
  832.2 7.5 copy-start.1
  832.2 9.8 %copy-start = (f32[768,3072]{1,0:T(8,128)S(1)}, f32[768,3072]{1,0:T(8,128)}, u32[]{:S(2)}) copy-start(f32[768,3072]{1,0:T(8,128)} %get-tuple-element.35) | copy-start | bytes 28311556
  839.7 7.1 slice-start
  842.0 6.0 slice-start.1
  842.0 6.2 slice-start.2
  842.0 10.8 %slice-start.3 = ((s8[4718592]{0:T(1024)(128)(4,1)}), s8[524288]{0:T(1024)(128)(4,1)S(1)}, s32[]{:S(2)}) async-start(s8[4718592]{0:T(1024)(128)(4,1)} %bitcast.17), calls=%async_computation.3 | async-start | bytes 1048576
  848.2 5.3 slice-start.4

commit v3 on v2

--- a/solution.py
+++ b/solution.py
@@ -12,6 +12,9 @@
 GELU_C = 0.7978845608028654
 GELU_A = 0.044715
 MESH_ID = pl.DeviceIdType.MESH
+LAG_MLP = 1
+GROUP = 4
+ROW_BLOCK = 32
 
 
 def dot_nn(lhs, rhs):
@@ -34,6 +37,10 @@
     scale = rms_scale(vals)
     inner = jnp.mean(vals * cotangent, axis=-1, keepdims=True)
     return scale * (cotangent - vals * (scale * scale * inner))
+
+
+def row_blocks(count):
+    return [pl.ds(start, ROW_BLOCK) for start in range(0, count, ROW_BLOCK)]
 
 
 def causal_weights(scores_t, col_max, col_inv, scale):
@@ -69,36 +76,57 @@
     return jnp.concatenate([upper, lower], axis=0)
 
 
-def forward_layer(dims, act_ref, wqkv, wout, wup, wdown, n1_ref, qkv_ref, stat_ref, ctx_ref, hid_ref, n2_ref, gp_ref, up_ref, out_ref, flush):
+def forward_layer(dims, act_ref, wqkv, wout, wup, wdown, n1_ref, qkv_ref, stat_ref, ctx_ref, hid_ref, n2_ref, gp_ref, up_ref, out_ref, flush, n1t_s, score_s, prob_s, acc_s, ready):
     heads, hdim, ffn_tile = dims
     width = heads * hdim
     ffn = wdown.shape[0]
     scale = hdim ** -0.5
-    act32 = act_ref[...].astype(jnp.float32)
-    normed1 = (act32 * rms_scale(act32)).astype(jnp.bfloat16)
-    n1_ref[...] = normed1
-    qkv_ref[...] = dot_nt(wqkv[...], normed1).astype(jnp.bfloat16)
-    flush(0)
-
-    def head_body(h, carry):
-        q_rows = pl.ds(pl.multiple_of(h * hdim, hdim), hdim)
-        k_rows = pl.ds(pl.multiple_of(width + h * hdim, hdim), hdim)
-        v_rows = pl.ds(pl.multiple_of(2 * width + h * hdim, hdim), hdim)
-        scores_t = dot_tn(qkv_ref[k_rows, :], qkv_ref[q_rows, :])
-        blocks, stats = causal_weights(scores_t, None, None, scale)
+    for rows in row_blocks(act_ref.shape[0]):
+        act32 = act_ref[rows, :].astype(jnp.float32)
+        n1_ref[rows, :] = (act32 * rms_scale(act32)).astype(jnp.bfloat16)
+    n1t_s[...] = n1_ref[...].T
+    ready(0)
+
+    def rows_of(h):
+        return tuple(pl.ds(part * width + h * hdim, hdim) for part in range(3))
+
+    def project(h):
+        rows = rows_of(h)
+        stacked = jnp.concatenate([wqkv[r, :] for r in rows], axis=0)
+        proj = dot_nn(stacked, n1t_s[...]).astype(jnp.bfloat16)
+        for part, r in enumerate(rows):
+            qkv_ref[r, :] = proj[part * hdim:(part + 1) * hdim]
+
+    def score(h):
+        rows = rows_of(h)
+        score_s[h % 3] = dot_tn(qkv_ref[rows[1], :], qkv_ref[rows[0], :])
+
+    def soften(h):
+        blocks, stats = causal_weights(score_s.at[h % 3], None, None, scale)
         stat_ref[h, 0:1, :] = stats[0]
         stat_ref[h, 1:2, :] = stats[1]
-        ctx_ref[q_rows, :] = dot_nn(qkv_ref[v_rows, :], assemble(blocks, jnp.bfloat16)).astype(jnp.bfloat16)
-        return carry
-
-    lax.fori_loop(0, heads, head_body, 0, unroll=True)
-    attn = dot_tn(ctx_ref[...], wout[...])
-    hid16 = (act_ref[...].astype(jnp.float32) + attn).astype(jnp.bfloat16)
-    hid_ref[...] = hid16
-    hid32 = hid16.astype(jnp.float32)
-    normed2 = (hid32 * rms_scale(hid32)).astype(jnp.bfloat16)
-    n2_ref[...] = normed2
+        prob_s[h % 2] = assemble(blocks, jnp.bfloat16)
+
+    def mix(h):
+        rows = rows_of(h)
+        ctx_ref[rows[0], :] = dot_nn(qkv_ref[rows[2], :], prob_s[h % 2]).astype(jnp.bfloat16)
+
+    for step in range(heads + 5):
+        for lag, action in ((0, project), (2, score), (4, soften), (5, mix)):
+            h = step - lag
+            if 0 <= h < heads:
+                action(h)
+    flush(0)
+    ready(1)
+    acc_s[...] = dot_tn(ctx_ref[...], wout[...])
+    for rows in row_blocks(act_ref.shape[0]):
+        hid16 = (act_ref[rows, :].astype(jnp.float32) + acc_s[rows, :]).astype(jnp.bfloat16)
+        hid_ref[rows, :] = hid16
+        hid32 = hid16.astype(jnp.float32)
+        n2_ref[rows, :] = (hid32 * rms_scale(hid32)).astype(jnp.bfloat16)
+    normed2 = n2_ref[...]
     flush(1)
+    ready(2)
     for tile in range(ffn // ffn_tile):
         cols = pl.ds(tile * ffn_tile, ffn_tile)
         pre = dot_nn(normed2, wup[:, cols])
@@ -106,17 +134,20 @@
         tanh = jnp.tanh(pre * (GELU_C + (GELU_C * GELU_A) * (pre * pre)))
         up_ref[:, cols] = (pre * (0.5 + 0.5 * tanh)).astype(jnp.bfloat16)
     flush(2)
-    down = dot_nn(up_ref[...], wdown[...])
-    out_ref[...] = (hid_ref[...].astype(jnp.float32) + down).astype(jnp.bfloat16)
-
-
-def backward_layer(dims, grad_ref, act_ref, wqkv, wout, wup, wdown, qkv_ref, stat_ref, hid_ref, gp_ref, dpre_ref, dhid_ref, dctx_ref, dqkv_ref, dact_ref, flush):
+    ready(3)
+    acc_s[...] = dot_nn(up_ref[...], wdown[...])
+    for rows in row_blocks(act_ref.shape[0]):
+        out_ref[rows, :] = (hid_ref[rows, :].astype(jnp.float32) + acc_s[rows, :]).astype(jnp.bfloat16)
+
+
+def backward_layer(dims, grad_ref, act_ref, wqkv, wout, wup, wdown, qkv_ref, stat_ref, hid_ref, gp_ref, dpre_ref, dhid_ref, dctx_ref, dqkv_ref, dact_ref, flush, acc_s, dhid_s32, dhidt_s, score_s, dprob_s, prob_s, dscore_s):
     heads, hdim, ffn_tile = dims
     width = heads * hdim
     ffn = wdown.shape[0]
     scale = hdim ** -0.5
     grad16 = grad_ref[...]
-    for tile in range(ffn // ffn_tile):
+
+    def slope(tile):
         cols = pl.ds(tile * ffn_tile, ffn_tile)
         dup = dot_nt(grad16, wdown[cols, :])
         pre = gp_ref[:, cols]
@@ -125,40 +156,80 @@
         half = 0.5 + 0.5 * tanh
         bend = (half * (1.0 - half)) * (pre * (2.0 * GELU_C + (6.0 * GELU_C * GELU_A) * pre_sq))
         dpre_ref[:, cols] = (dup * (half + bend)).astype(jnp.bfloat16)
+
+    def gather(tile):
+        cols = pl.ds(tile * ffn_tile, ffn_tile)
+        part = dot_nt(dpre_ref[:, cols], wup[:, cols])
+        if tile == 0:
+            acc_s[...] = part
+        else:
+            acc_s[...] += part
+
+    tiles = ffn // ffn_tile
+    for step in range(tiles + LAG_MLP):
+        if step < tiles:
+            slope(step)
+        if step >= LAG_MLP:
+            gather(step - LAG_MLP)
     flush(0)
-    dnormed2 = dot_nt(dpre_ref[...], wup[...])
-    dhid32 = grad_ref[...].astype(jnp.float32) + rms_vjp(hid_ref[...].astype(jnp.float32), dnormed2)
-    dhid16 = dhid32.astype(jnp.bfloat16)
-    dhid_ref[...] = dhid16
+    for rows in row_blocks(act_ref.shape[0]):
+        dhid32 = grad_ref[rows, :].astype(jnp.float32) + rms_vjp(hid_ref[rows, :].astype(jnp.float32), acc_s[rows, :])
+        dhid_s32[rows, :] = dhid32
+        dhid_ref[rows, :] = dhid32.astype(jnp.bfloat16)
+    dhidt_s[...] = dhid_ref[...].T
     flush(1)
-    dctx_ref[...] = dot_nt(wout[...], dhid16).astype(jnp.bfloat16)
-
-    def head_body(h, carry):
-        q_rows = pl.ds(pl.multiple_of(h * hdim, hdim), hdim)
-        k_rows = pl.ds(pl.multiple_of(width + h * hdim, hdim), hdim)
-        v_rows = pl.ds(pl.multiple_of(2 * width + h * hdim, hdim), hdim)
-        query_t = qkv_ref[q_rows, :]
-        keys_t = qkv_ref[k_rows, :]
-        dctx_t = dctx_ref[q_rows, :]
-        scores_t = dot_tn(keys_t, query_t)
-        probs, _ = causal_weights(scores_t, stat_ref[h, 0:1, :], stat_ref[h, 1:2, :], scale)
-        dprobs = dot_tn(qkv_ref[v_rows, :], dctx_t)
+
+    def rows_of(h):
+        return tuple(pl.ds(part * width + h * hdim, hdim) for part in range(3))
+
+    def project(h):
+        rows = rows_of(h)[0]
+        dctx_ref[rows, :] = dot_nn(wout[rows, :], dhidt_s[...]).astype(jnp.bfloat16)
+
+    def score(h):
+        rows = rows_of(h)
+        score_s[h % 3] = dot_tn(qkv_ref[rows[1], :], qkv_ref[rows[0], :])
+        dprob_s[h % 3] = dot_tn(qkv_ref[rows[2], :], dctx_ref[rows[0], :])
+
+    def soften(h):
+        probs, _ = causal_weights(score_s.at[h % 3], stat_ref[h, 0:1, :], stat_ref[h, 1:2, :], scale)
+        dprobs = dprob_s.at[h % 3]
         half = dprobs.shape[0] // 2
         d_ul, d_ur, d_lr = dprobs[:half, :half], dprobs[:half, half:], dprobs[half:, half:]
         p_ul, p_ur, p_lr = probs
         delta_l = jnp.sum(d_ul * p_ul, axis=0, keepdims=True)
         delta_r = jnp.sum(d_ur * p_ur, axis=0, keepdims=True) + jnp.sum(d_lr * p_lr, axis=0, keepdims=True)
-        dscores = assemble((p_ul * (d_ul - delta_l) * scale, p_ur * (d_ur - delta_r) * scale, p_lr * (d_lr - delta_r) * scale), jnp.bfloat16)
-        dqkv_ref[v_rows, :] = dot_nt(dctx_t, assemble(probs, jnp.bfloat16)).astype(jnp.bfloat16)
-        dqkv_ref[q_rows, :] = dot_nn(keys_t, dscores).astype(jnp.bfloat16)
-        dqkv_ref[k_rows, :] = dot_nt(query_t, dscores).astype(jnp.bfloat16)
-        return carry
-
-    lax.fori_loop(0, heads, head_body, 0, unroll=True)
+        prob_s[h % 2] = assemble(probs, jnp.bfloat16)
+        dscore_s[h % 2] = assemble((p_ul * (d_ul - delta_l) * scale, p_ur * (d_ur - delta_r) * scale, p_lr * (d_lr - delta_r) * scale), jnp.bfloat16)
+
+    def mix(h):
+        rows = rows_of(h)
+        dqkv_ref[rows[2], :] = dot_nt(dctx_ref[rows[0], :], prob_s[h % 2]).astype(jnp.bfloat16)
+        dqkv_ref[rows[0], :] = dot_nn(qkv_ref[rows[1], :], dscore_s[h % 2]).astype(jnp.bfloat16)
+        dqkv_ref[rows[1], :] = dot_nt(qkv_ref[rows[0], :], dscore_s[h % 2]).astype(jnp.bfloat16)
+
+    def collect(first, count):
+        spans = [pl.ds(part * width + first * hdim, count * hdim) for part in range(3)]
+        part = dot_tn(jnp.concatenate([dqkv_ref[r, :] for r in spans], axis=0), jnp.concatenate([wqkv[r, :] for r in spans], axis=0))
+        if first == 0:
+            acc_s[...] = part
+        else:
+            acc_s[...] += part
+
+    group = min(GROUP, heads)
+    for step in range(heads + 5):
+        for lag, action in ((0, project), (2, score), (4, soften), (5, mix)):
+            h = step - lag
+            if 0 <= h < heads:
+                action(h)
+        done = step - 6
+        if done >= 0 and done % group == group - 1 and done < heads - group:
+            collect(done - group + 1, group)
     flush(2)
-    dnormed1 = dot_tn(dqkv_ref[...], wqkv[...])
-    dact = dhid32 + rms_vjp(act_ref[...].astype(jnp.float32), dnormed1)
-    dact_ref[...] = dact.astype(jnp.bfloat16)
+    collect(heads - group, group)
+    for rows in row_blocks(act_ref.shape[0]):
+        dact = dhid_s32[rows, :] + rms_vjp(act_ref[rows, :].astype(jnp.float32), acc_s[rows, :])
+        dact_ref[rows, :] = dact.astype(jnp.bfloat16)
 
 
 class placement:
@@ -189,7 +260,7 @@
     wqkv, wout, wup, wdown, act, grad, out_s, dact_s,
     n1_s, n2_s, up_s, ctx_s, qkv_s, gp_s, hid_s, stat_s,
     dpre_s, dhid_s, dctx_s, dqkv_s,
-    w_sem, in_sem, act_sem, grad_sem, fout_sem, bin_sem, bout_sem, fsend_sem, bsend_sem, loss_acc, loss_sem, dx_sem,
+    w_sem, in_sem, act_sem, grad_sem, fout_sem, bin_sem, bout_sem, fsend_sem, bsend_sem, loss_acc, loss_sem, dx_sem, n1t_s, score_s, prob_s, dprob_s, dscore_s, acc_s, dhid_s32,
 ):
     n_stages, n_seq, tokens, grad_scale, dims = cfg
     here = placement(n_stages)
@@ -257,14 +328,13 @@
     each_seq(feeds_last, lambda m: give_target(m).start())
     loss_acc[...] = jnp.zeros_like(loss_acc)
 
-    @pl.when(own_weights)
-    def _():
-        for idx in range(4):
+    def await_weight(idx):
+        @pl.when(own_weights)
+        def _():
             load_weight(idx).wait()
 
-    @pl.when(jnp.logical_not(own_weights))
-    def _():
-        for idx in range(4):
+        @pl.when(jnp.logical_not(own_weights))
+        def _():
             give_weight(idx).wait_recv()
 
     def send_act(m, slot):
@@ -345,10 +415,19 @@
             def _():
                 send_act(m, slot).wait_recv()
 
-            forward_layer(
-                dims, act.at[m], wqkv, wout, wup, wdown, n1_s.at[slot], qkv_s.at[slot], stat_s.at[slot],
-                ctx_s.at[slot], hid_s.at[slot], n2_s.at[slot], gp_s.at[slot], up_s.at[slot], out_s.at[slot],
-                flusher(fout_copies(m, slot)))
+            def run_forward(ready):
+                forward_layer(
+                    dims, act.at[m], wqkv, wout, wup, wdown, n1_s.at[slot], qkv_s.at[slot], stat_s.at[slot],
+                    ctx_s.at[slot], hid_s.at[slot], n2_s.at[slot], gp_s.at[slot], up_s.at[slot], out_s.at[slot],
+                    flusher(fout_copies(m, slot)), n1t_s, score_s, prob_s, acc_s, ready)
+
+            @pl.when(m == 0)
+            def _():
+                run_forward(await_weight)
+
+            @pl.when(m > 0)
+            def _():
+                run_forward(lambda idx: None)
 
             @pl.when(jnp.logical_not(is_last))
             def _():
@@ -364,13 +443,12 @@
 
             @pl.when(is_last)
             def _():
-                error = out_s[slot].astype(jnp.float32) - grad[m].astype(jnp.float32)
-                square = error * error
-                total = square[0:8]
-                for row in range(8, tokens, 8):
-                    total = total + square[row:row + 8]
-                loss_acc[...] += total
-                grad[m] = (error * grad_scale).astype(jnp.bfloat16)
+                for start in range(0, tokens, 32):
+                    rows = pl.ds(start, 32)
+                    error = out_s[slot, rows, :].astype(jnp.float32) - grad[m, rows, :].astype(jnp.float32)
+                    square = error * error
+                    loss_acc[...] += (square[0:8] + square[8:16]) + (square[16:24] + square[24:32])
+                    grad[m, rows, :] = (error * grad_scale).astype(jnp.bfloat16)
 
         @pl.when(in_range(bwd_m))
         def _():
@@ -387,7 +465,7 @@
             backward_layer(
                 dims, grad.at[m], act.at[m], wqkv, wout, wup, wdown, qkv_s.at[saved], stat_s.at[saved], hid_s.at[saved],
                 gp_s.at[saved], dpre_s.at[slot], dhid_s.at[slot], dctx_s, dqkv_s.at[slot], dact_s.at[slot],
-                flusher(bout_copies(m, slot)))
+                flusher(bout_copies(m, slot)), acc_s, dhid_s32, n1t_s, score_s, dprob_s, prob_s, dscore_s)
 
             @pl.when(jnp.logical_not(is_first))
             def _():
@@ -511,6 +589,8 @@
         pltpu.SemaphoreType.DMA((2, 8)), pltpu.SemaphoreType.DMA((4,)), pltpu.SemaphoreType.DMA((2, 4)),
         pltpu.SemaphoreType.DMA((2,)), pltpu.SemaphoreType.DMA((2,)),
         pltpu.VMEM((8, width), f32), pltpu.SemaphoreType.DMA((2,)), pltpu.SemaphoreType.DMA((n_seq,)),
+        pltpu.VMEM((width, tokens), bf16), pltpu.VMEM((3, tokens, tokens), f32), pltpu.VMEM((2, tokens, tokens), bf16),
+        pltpu.VMEM((3, tokens, tokens), f32), pltpu.VMEM((2, tokens, tokens), bf16), pltpu.VMEM((tokens, width), f32), pltpu.VMEM((tokens, width), f32),
     ]
     linear = 2 * total * (wqkv.size + wout.size + wup.size + wdown.size)
     return pl.pallas_call(
@@ -738,34 +818,38 @@
                 arrival(kind, num, 1 - pair, unit).wait_recv()
                 arrival(kind, num, 1 - pair, unit).start()
 
-    def round_body(num, carry):
+    def kind_at(pos):
+        late = jnp.where(pos == 4, 2, jnp.where(pos == 5, 3, jnp.where(pos == 6, 1, 0)))
+        return jnp.where(pos < 4, pos, late)
+
+    def num_at(pos):
+        return jnp.where(pos < 4, 0, 1)
+
+    n_steps = 2 * n_kinds
+
+    def step_body(pos, carry):
         for kind in range(n_kinds):
-            first_half(kind, num)
-            if kind >= 1:
-                second_half(kind - 1, num)
-            else:
-                @pl.when(num > 0)
-                def _():
-                    second_half(n_kinds - 1, num - 1)
-            if kind >= 2:
-                pass_on(kind - 2, num)
-            else:
-                @pl.when(num > 0)
-                def _():
-                    pass_on(kind + 2, num - 1)
-        for idx in range(2):
-            if idx < len(spans):
-                @pl.when(num == idx)
-                def _():
-                    spread_round(idx)
+            @pl.when((pos < n_steps) & (kind_at(pos) == kind))
+            def _():
+                first_half(kind, num_at(pos))
+
+        for kind in range(n_kinds):
+            @pl.when((pos >= 1) & (pos < n_steps + 1) & (kind_at(pos - 1) == kind))
+            def _():
+                second_half(kind, num_at(pos - 1))
+
+        for kind in range(n_kinds):
+            @pl.when((pos >= 2) & (kind_at(pos - 2) == kind))
+            def _():
+                pass_on(kind, num_at(pos - 2))
+
+        for idx in range(len(spans) + 1):
+            @pl.when(pos == 3 * idx)
+            def _():
+                spread_round(idx)
         return carry
 
-    lax.fori_loop(0, 2, round_body, 0)
-    second_half(n_kinds - 1, 1)
-    for idx in range(min(2, len(spans)), len(spans) + 1):
-        spread_round(idx)
-    pass_on(n_kinds - 2, 1)
-    pass_on(n_kinds - 1, 1)
+    lax.fori_loop(0, n_steps + 2, step_body, 0)
 
     for idx in range(3):
         loss_arrival(idx).wait_recv()

time: 867 us -> 793 us (0.915); the launches traced: 857 us -> 793 us
  Pallas kernels: 830 us -> 766 us
    pallas_call x1, Pallas kernels: 484 us -> 416 us  [run_pipeline(): pl.pallas_call(functools.partial(pipeline_kernel, (n_stages, n_seq, token...]
where the time goes in v3:
time: 793 us
  Pallas kernels  766 us (97%)
  local copies, waits for them, and re-layouts  23.5 us (3%)
    pallas_call x1, Pallas kernels, run_pipeline(): pl.pallas_call(functools.partial(pipeline_kernel, (n_stages, n_seq, token...  416 us
    pallas_call x1, Pallas kernels, sum_gradients(): pl.pallas_call(functools.partial(reduce_kernel, (n_stages,)), out_shape=[...  349 us
    unnamed x19, local copies, waits for them, and re-layouts  23.5 us

profile of v3, /device:TPU:97, one launch (start us, length us, event | category | flops | bytes accessed | tf_op | source)
XLA Modules:
  0.0 792.8 jit_solution(13736473136259664892)
XLA Ops:
  0.6 416.3 %stage_pipeline.1 = (f32[8,128]{1,0:T(8,128)}, bf16[3072,768]{1,0:T(8,128)(2,1)}, bf16[3072,768]{1,0:T(8,128)(2,1)}, bf16[3072,3072]{1,0:T(8,128)(2,1)}, bf16[76...) custom-call(bf16[12,256,768]{2,1,0:T(8,128)(2,1)} %bitcast.21, ...), custom_call_target="tpu_custom_call" | custom-call | flops 130459631616 | bytes 209715200 | tf_op jit(solution)/shard_map/stage_pipeline/pallas_call | solution.py:596
  417.0 349.3 %gradient_sums.1 = (f32[8,128]{1,0:T(8,128)}, f32[768,768]{1,0:T(8,128)}, f32[2304,768]{1,0:T(8,128)}, f32[3072,768]{1,0:T(8,128)}, f32[768,3072]{1,0:T(8,128)}, /*index=5*/bf16[12,256,768]{2,1,0:T(8,128)(2,1)}) custom-call(f32[8,128]{1,0:T(8,128)} %get-tuple-element.22.loss_hbm, ...), custom_call_target="tpu_custom_call", output_to_operand_aliasing={{5}: (9, {})} | custom-call | flops 43486543872 | bytes 157286400 | tf_op jit(solution)/shard_map/gradient_sums/pallas_call | solution.py:914
  766.2 1.3 reduce_sum.9
  768.2 0.0 copy-start.1
  768.2 0.0 copy-start
  768.2 7.5 copy.19
  775.7 0.0 copy-done.1
  775.7 0.0 slice-start
  775.7 1.4 copy.20
  777.1 0.9 copy-done
  778.0 0.0 slice-start.1
  778.0 0.0 slice-start.2
  778.0 0.0 slice-start.3
  778.0 4.8 copy.21
  782.8 0.0 slice-done
  782.8 1.2 slice-done.1
  783.9 0.2 slice-done.2
  784.2 0.0 slice-start.4
  784.2 4.6 copy.22
  788.8 0.0 slice-done.3
  788.8 0.7 slice-done.4
  789.5 2.2 copy.23
  (2 shorter events, 0.0 us)
Async XLA Ops:
  768.2 7.5 copy-start.1
  768.2 9.8 %copy-start = (f32[768,3072]{1,0:T(8,128)S(1)}, f32[768,3072]{1,0:T(8,128)}, u32[]{:S(2)}) copy-start(f32[768,3072]{1,0:T(8,128)} %get-tuple-element.35) | copy-start | bytes 28311556
  775.7 7.1 slice-start
  778.0 6.0 slice-start.1
  778.0 6.2 slice-start.2
  778.0 10.8 %slice-start.3 = ((s8[4718592]{0:T(1024)(128)(4,1)}), s8[524288]{0:T(1024)(128)(4,1)S(1)}, s32[]{:S(2)}) async-start(s8[4718592]{0:T(1024)(128)(4,1)} %bitcast.17), calls=%async_computation.3 | async-start | bytes 1048576
  784.2 5.3 slice-start.4

commit v4 on v3

--- a/solution.py
+++ b/solution.py
@@ -653,28 +653,49 @@
         dst = kinds[kind][8]
         return dst.at[:, part] if kinds[kind][0] == 'wide' else dst.at[part, :]
 
+    tile = min(256, out_res.shape[1])
+    n_tiles = out_res.shape[1] // tile
+
+    def tile_at(kind, n):
+        span = pl.ds(pl.multiple_of(n * tile, tile), tile)
+        return (span, slice(None)) if kinds[kind][0] == 'wide' else (slice(None), span)
+
+    def each_tile(action):
+        def body(n, carry):
+            action(n)
+            return carry
+        lax.fori_loop(0, n_tiles, body, 0)
+
     def give(kind, other, num):
         return pltpu.make_async_remote_copy(
             src_ref=kinds[kind][5].at[other], dst_ref=kinds[kind][6].at[num, other], send_sem=give_sem.at[kind, other],
             recv_sem=core_sem.at[kind, num, other], device_id=here.mate_id, device_id_type=MESH_ID)
 
-    def send_row(kind, num):
-        return pltpu.make_async_remote_copy(
-            src_ref=kinds[kind][6].at[num, 1], dst_ref=kinds[kind][7].at[num], send_sem=row_send.at[kind, num],
-            recv_sem=row_recv.at[kind, num], device_id=pair_id, device_id_type=MESH_ID)
-
-    def put(kind, num, target, device_id):
-        return pltpu.make_async_remote_copy(
-            src_ref=kinds[kind][7].at[num], dst_ref=out_view(kind, pair, core, num), send_sem=put_send.at[target, kind, num],
-            recv_sem=put_recv.at[pair, core, kind, num], device_id=device_id, device_id_type=MESH_ID)
+    def send_row(kind, num, n):
+        at = tile_at(kind, n)
+        return pltpu.make_async_remote_copy(
+            src_ref=kinds[kind][6].at[(num, 1) + at], dst_ref=kinds[kind][7].at[(num,) + at], send_sem=row_send.at[kind, num, n],
+            recv_sem=row_recv.at[kind, num, n], device_id=pair_id, device_id_type=MESH_ID)
+
+    def put_view(kind, member, unit, num, n):
+        part = piece(kind, member, unit, num)
+        span = pl.ds(pl.multiple_of(n * tile, tile), tile)
+        dst = kinds[kind][8]
+        return dst.at[span, part] if kinds[kind][0] == 'wide' else dst.at[part, span]
+
+    def put(kind, num, n, target, device_id):
+        return pltpu.make_async_remote_copy(
+            src_ref=kinds[kind][7].at[(num,) + tile_at(kind, n)], dst_ref=put_view(kind, pair, core, num, n),
+            send_sem=put_send.at[target, kind, num, n], recv_sem=put_recv.at[pair, core, kind, num, n],
+            device_id=device_id, device_id_type=MESH_ID)
 
     def keep(kind, num):
         return pltpu.make_async_copy(kinds[kind][7].at[num], out_view(kind, pair, core, num), store_sem.at[kind, num])
 
-    def arrival(kind, num, member, unit):
-        view = out_view(kind, member, unit, num)
-        return pltpu.make_async_remote_copy(
-            src_ref=view, dst_ref=view, send_sem=pass_send.at[unit, kind, num], recv_sem=put_recv.at[member, unit, kind, num],
+    def arrival(kind, num, n, member, unit):
+        view = put_view(kind, member, unit, num, n)
+        return pltpu.make_async_remote_copy(
+            src_ref=view, dst_ref=view, send_sem=pass_send.at[unit, kind, num, n], recv_sem=put_recv.at[member, unit, kind, num, n],
             device_id=across_home_id, device_id_type=MESH_ID)
 
     def load_resident(kind):
@@ -750,7 +771,7 @@
             def _():
                 spread(idx).start()
 
-    def product(kind, turn, num, sink, base):
+    def product(kind, turn, num, sink, base, before=None, after=None):
         form, _, res, _, buf = kinds[kind][:5]
         read_piece(kind, turn, num).wait()
         if turn < 3:
@@ -760,22 +781,25 @@
             def _():
                 read_piece(kind, 0, 1).start()
         fed = buf.at[turn % 2]
-        tile = min(256, res.shape[1])
-
-        def body(n, carry):
+
+        def body(n):
+            at = tile_at(kind, n)
             span = pl.ds(pl.multiple_of(n * tile, tile), tile)
+            if before is not None:
+                before(n)
             if form == 'rows':
-                part, at = dot_nn(fed[...], res[:, span]), (slice(None), span)
+                part = dot_nn(fed[...], res[:, span])
             elif form == 'tall':
-                part, at = dot_tn(fed[...], res[:, span]), (slice(None), span)
+                part = dot_tn(fed[...], res[:, span])
             else:
-                part, at = dot_tn(res[:, span], fed[...]), (span, slice(None))
+                part = dot_tn(res[:, span], fed[...])
             for ref in base:
                 part = part + ref[at]
             sink[at] = part
-            return carry
-
-        lax.fori_loop(0, res.shape[1] // tile, body, 0)
+            if after is not None:
+                after(n)
+
+        each_tile(body)
 
     def first_half(kind, num):
         give_buf, core_buf = kinds[kind][5:7]
@@ -792,31 +816,35 @@
             product(kind, turn, num, give_buf.at[other], ())
             give(kind, other, num).start()
         give(kind, 1, num).wait_recv()
-        product(kind, 2, num, core_buf.at[num, 1], (core_buf.at[num, 1],))
-        send_row(kind, num).start()
+        product(kind, 2, num, core_buf.at[num, 1], (core_buf.at[num, 1],), after=lambda n: send_row(kind, num, n).start())
 
     def second_half(kind, num):
         core_buf, row_buf = kinds[kind][6:8]
         give(kind, 0, num).wait_recv()
-        send_row(kind, num).wait_recv()
-        product(kind, 3, num, row_buf.at[num], (core_buf.at[num, 0], row_buf.at[num]))
-        put(kind, num, 1, pair_home_id).start()
-        put(kind, num, 2, across_home_id).start()
+
+        def after(n):
+            put(kind, num, n, 1, pair_home_id).start()
+            put(kind, num, n, 2, across_home_id).start()
+
+            @pl.when(jnp.logical_not(is_home))
+            def _():
+                put(kind, num, n, 0, home_id).start()
+
+        product(kind, 3, num, row_buf.at[num], (core_buf.at[num, 0], row_buf.at[num]),
+                before=lambda n: send_row(kind, num, n).wait_recv(), after=after)
 
         @pl.when(is_home)
         def _():
             keep(kind, num).start()
-
-        @pl.when(jnp.logical_not(is_home))
-        def _():
-            put(kind, num, 0, home_id).start()
 
     def pass_on(kind, num):
         @pl.when(is_home)
         def _():
-            for unit in range(2):
-                arrival(kind, num, 1 - pair, unit).wait_recv()
-                arrival(kind, num, 1 - pair, unit).start()
+            def go(n):
+                for unit in range(2):
+                    arrival(kind, num, n, 1 - pair, unit).wait_recv()
+                    arrival(kind, num, n, 1 - pair, unit).start()
+            each_tile(go)
 
     def kind_at(pos):
         late = jnp.where(pos == 4, 2, jnp.where(pos == 5, 3, jnp.where(pos == 6, 1, 0)))
@@ -860,23 +888,29 @@
 
     for kind in range(n_kinds):
         for num in range(2):
+            def settle(n):
+                @pl.when(is_home)
+                def _():
+                    arrival(kind, num, n, pair, 1 - core).wait_recv()
+                    for unit in range(2):
+                        arrival(kind, num, n, 1 - pair, unit).wait_send()
+
+                @pl.when(jnp.logical_not(is_home))
+                def _():
+                    for member in range(2):
+                        for unit in range(2):
+                            arrival(kind, num, n, member, unit).wait_recv()
+                    put(kind, num, n, 0, home_id).wait_send()
+
+                send_row(kind, num, n).wait_send()
+                put(kind, num, n, 1, pair_home_id).wait_send()
+                put(kind, num, n, 2, across_home_id).wait_send()
+
+            each_tile(settle)
+
             @pl.when(is_home)
             def _():
-                arrival(kind, num, pair, 1 - core).wait_recv()
                 keep(kind, num).wait()
-                for unit in range(2):
-                    arrival(kind, num, 1 - pair, unit).wait_send()
-
-            @pl.when(jnp.logical_not(is_home))
-            def _():
-                for member in range(2):
-                    for unit in range(2):
-                        arrival(kind, num, member, unit).wait_recv()
-                put(kind, num, 0, home_id).wait_send()
-
-            send_row(kind, num).wait_send()
-            put(kind, num, 1, pair_home_id).wait_send()
-            put(kind, num, 2, across_home_id).wait_send()
         for other in range(2):
             give(kind, other, 1).wait_send()
     for idx in range(3):
@@ -896,6 +930,7 @@
     vmem_spec = pl.BlockSpec(memory_space=pltpu.VMEM)
     out_shapes = [(loss_part.shape, f32), ((width, width), f32), ((3 * width, width), f32), ((ffn, width), f32), ((width, ffn), f32), (dx.shape, bf16)]
     n_spans = n_stages.bit_length() - 1
+    n_tiles = max(1, width // 256)
     pieces = ((small, width), (mid, width), (big, width), (width, big))
     dma = pltpu.SemaphoreType.DMA
     scratch = [pltpu.VMEM((total, width), bf16)] * 4 + [
@@ -907,8 +942,8 @@
     scratch += [pltpu.VMEM((2,) + p, f32) for p in pieces]
     scratch += [
         pltpu.VMEM((4,) + loss_part.shape, f32),
-        dma((4,)), dma((4, 2)), dma((4, 2)), dma((4, 2, 2)), dma((4, 2)), dma((4, 2)), dma((3, 4, 2)), dma((2, 2, 4, 2)),
-        dma((2, 4, 2)), dma((4, 2)), dma((2, n_spans)), dma((3,)), dma((3,)), dma(()),
+        dma((4,)), dma((4, 2)), dma((4, 2)), dma((4, 2, 2)), dma((4, 2, n_tiles)), dma((4, 2, n_tiles)),
+        dma((3, 4, 2, n_tiles)), dma((2, 2, 4, 2, n_tiles)), dma((2, 4, 2, n_tiles)), dma((4, 2)), dma((2, n_spans)), dma((3,)), dma((3,)), dma(()),
     ]
     flops = 2 * total * width * (4 * width + 2 * ffn)
     return pl.pallas_call(
@@ -924,6 +959,44 @@
     )(loss_part, ctx_t, dhid, dqkv_t, n1, upper, grads, n2, dpre, dx)
 
 
+def settle_kernel(plan, loss_factor, loss_in, *refs):
+    count = len(plan)
+    sources, loss_ref, results = refs[:count], refs[count], refs[count + 1:2 * count + 1]
+    holds, sem = refs[2 * count + 1:-1], refs[-1]
+    copies = []
+    for src, hold, dst, parts in zip(sources, holds, results, plan):
+        lead = src.shape[0] // parts
+        for idx in range(parts):
+            part = pl.ds(idx * lead, lead)
+            num = len(copies)
+            copies.append((
+                pltpu.make_async_copy(src.at[part], hold.at[part], sem.at[0, num]),
+                pltpu.make_async_copy(hold.at[part], dst.at[part], sem.at[1, num])))
+    for read, _ in copies:
+        read.start()
+    loss_ref[0] = loss_factor * jnp.sum(loss_in[...])
+    for read, write in copies:
+        read.wait()
+        write.start()
+    for _, write in copies:
+        write.wait()
+
+
+def settle(loss_factor, loss_sum, arrays):
+    plan = tuple(next(p for p in (4, 3, 2, 1) if arr.shape[0] % (16 * p) == 0 or p == 1 or (arr.ndim == 3 and arr.shape[0] % p == 0)) for arr in arrays)
+    any_spec = pl.BlockSpec(memory_space=pl.ANY)
+    outs = pl.pallas_call(
+        functools.partial(settle_kernel, plan, loss_factor),
+        out_shape=[jax.ShapeDtypeStruct((1,), jnp.float32)] + [jax.ShapeDtypeStruct(arr.shape, arr.dtype) for arr in arrays],
+        in_specs=[pl.BlockSpec(memory_space=pltpu.VMEM)] + [any_spec] * len(arrays),
+        out_specs=[pl.BlockSpec(memory_space=pltpu.SMEM)] + [any_spec] * len(arrays),
+        scratch_shapes=[pltpu.VMEM(arr.shape, arr.dtype) for arr in arrays] + [pltpu.SemaphoreType.DMA((2, sum(plan)))],
+        compiler_params=pltpu.CompilerParams(vmem_limit_bytes=60 * 2 ** 20),
+        name='settle_results',
+    )(loss_sum, *arrays)
+    return outs[0], outs[1:]
+
+
 def solution(mesh):
     n_stages = mesh.shape['stage']
     n_data = mesh.shape['data']
@@ -940,9 +1013,9 @@
             n_stages, grad_scale, embeds.reshape(flat), targets.reshape(flat), w_qkv.reshape(3 * width, width),
             w_out.reshape(width, width), w_up[0], w_down[0], heads, hdim)
         loss_part, n1, n2, upper, ctx_t, dqkv_t, dpre, dhid, grads, dx = outs[:10]
-        loss_sum, d_out, d_qkv, d_down, d_up, d_embeds = sum_gradients(
+        loss_sum, *sums = sum_gradients(
             n_stages, loss_part, ctx_t, dhid, dqkv_t, n1, upper, grads, n2, dpre, dx)
-        loss = (0.5 * loss_norm * jnp.sum(loss_sum)).reshape(1)
+        loss, (d_out, d_qkv, d_down, d_up, d_embeds) = settle(0.5 * loss_norm, loss_sum, sums)
         return (loss, d_qkv.reshape(w_qkv.shape), d_out.reshape(w_out.shape), d_up[None], d_down[None], d_embeds.reshape(embeds.shape))
 
     return jax.shard_map(per_device, mesh=mesh, in_specs=(act_spec, act_spec, weight_spec, weight_spec, weight_spec, weight_spec), out_specs=(P('rep'), weight_spec, weight_spec, weight_spec, weight_spec, act_spec), check_vma=False)

time: 793 us -> 774 us (0.976)
  local copies, waits for them, and re-layouts: 23.5 us -> 0 us
    pallas_call x0 -> x1, Pallas kernels: none -> 24 us  [settle(): pl.pallas_call(functools.partial(settle_kernel, plan, loss_factor), out_s...]
    unnamed x19 -> x0, local copies, waits for them, and re-layouts: 23.5 us -> none
    pallas_call x1, Pallas kernels: 349 us -> 332 us  [sum_gradients(): pl.pallas_call(functools.partial(reduce_kernel, (n_stages,)), out_shape=[...]
where the time goes in v4:
time: 774 us; the launch traced here: 773 us
  Pallas kernels  773 us (100%)
    pallas_call x1, Pallas kernels, run_pipeline(): pl.pallas_call(functools.partial(pipeline_kernel, (n_stages, n_seq, token...  416 us
    pallas_call x1, Pallas kernels, sum_gradients(): pl.pallas_call(functools.partial(reduce_kernel, (n_stages,)), out_shape=[...  332 us
    pallas_call x1, Pallas kernels, settle(): pl.pallas_call(functools.partial(settle_kernel, plan, loss_factor), out_s...  24 us

profile of v4, /device:TPU:97, one launch (start us, length us, event | category | flops | bytes accessed | tf_op | source)
XLA Modules:
  0.0 773.5 jit_solution(14396577484166069476)
XLA Ops:
  0.6 416.3 %stage_pipeline.1 = (f32[8,128]{1,0:T(8,128)}, bf16[3072,768]{1,0:T(8,128)(2,1)}, bf16[3072,768]{1,0:T(8,128)(2,1)}, bf16[3072,3072]{1,0:T(8,128)(2,1)}, bf16[76...) custom-call(bf16[12,256,768]{2,1,0:T(8,128)(2,1)} %bitcast.14, ...), custom_call_target="tpu_custom_call" | custom-call | flops 130459631616 | bytes 209715200 | tf_op jit(solution)/shard_map/stage_pipeline/pallas_call | solution.py:596
  417.0 332.4 %gradient_sums.1 = (f32[8,128]{1,0:T(8,128)}, f32[768,768]{1,0:T(8,128)}, f32[2304,768]{1,0:T(8,128)}, f32[3072,768]{1,0:T(8,128)}, f32[768,3072]{1,0:T(8,128)}, /*index=5*/bf16[12,256,768]{2,1,0:T(8,128)(2,1)}) custom-call(f32[8,128]{1,0:T(8,128)} %get-tuple-element.28.loss_hbm, ...), custom_call_target="tpu_custom_call", output_to_operand_aliasing={{5}: (9, {})} | custom-call | flops 43486543872 | bytes 157286400 | tf_op jit(solution)/shard_map/gradient_sums/pallas_call | solution.py:949
  749.3 24.0 %settle_results.1 = (f32[1]{0:T(128)}, f32[768,768]{1,0:T(8,128)}, f32[2304,768]{1,0:T(8,128)}, f32[3072,768]{1,0:T(8,128)}, f32[768,3072]{1,0:T(8,128)}, /*index=5*/bf16[12,256,768]{2,1,0:T(8,128)(2,1)}) custom-call(f32[8,128]{1,0:T(8,128)} %get-tuple-element.38.loss_in, f32[768,768]{1,0:T(8,128)} %get-tuple-element.39.refs_0_, ...), custom_call_target="tpu_custom_call" | custom-call | tf_op jit(solution)/shard_map/settle_results/pallas_call | solution.py:988

commit v5 on v4

--- a/solution.py
+++ b/solution.py
@@ -400,7 +400,7 @@
 
     def tick(t, carry):
         fwd_m = t - stage
-        bwd_m = t + stage - (2 * n_stages - 2)
+        bwd_m = t + 2 * stage - 3 * (n_stages - 1)
 
         @pl.when(in_range(fwd_m))
         def _():
@@ -517,7 +517,7 @@
 
         return carry
 
-    lax.fori_loop(0, n_seq + 2 * n_stages - 1, tick, 0)
+    lax.fori_loop(0, n_seq + 3 * (n_stages - 1) + 1, tick, 0)
 
     def send_loss():
         return pltpu.make_async_remote_copy(
@@ -706,9 +706,8 @@
 
     my_loss = pltpu.make_async_copy(loss_hbm, loss_sl.at[pipeline_id(row, core)], loss_in)
     my_loss.start()
-    for kind in range(n_kinds):
-        load_resident(kind).start()
-        read_piece(kind, 0, 0).start()
+    load_resident(0).start()
+    read_piece(0, 0, 0).start()
 
     source = here.upper
     rank = stage + source - 2 * source * core
@@ -746,6 +745,9 @@
             src_ref=slot, dst_ref=slot, send_sem=loss_send.at[idx], recv_sem=loss_recv.at[idx],
             device_id=loss_ids[idx][0], device_id_type=MESH_ID)
 
+    for kind in range(1, n_kinds):
+        load_resident(kind).start()
+        read_piece(kind, 0, 0).start()
     my_loss.wait()
     for idx in range(3):
         send_loss(idx).start()

time: 774 us -> 775 us (level)
    pallas_call x1, Pallas kernels: 332 us -> 345 us  [sum_gradients(): pl.pallas_call(functools.partial(reduce_kernel, (n_stages,)), out_shape=[...]
    pallas_call x1, Pallas kernels: 416 us -> 404 us  [run_pipeline(): pl.pallas_call(functools.partial(pipeline_kernel, (n_stages, n_seq, token...]
where the time goes in v5:
time: 775 us; the launch traced here: 774 us
  Pallas kernels  774 us (100%)
    pallas_call x1, Pallas kernels, run_pipeline(): pl.pallas_call(functools.partial(pipeline_kernel, (n_stages, n_seq, token...  404 us
    pallas_call x1, Pallas kernels, sum_gradients(): pl.pallas_call(functools.partial(reduce_kernel, (n_stages,)), out_shape=[...  345 us
    pallas_call x1, Pallas kernels, settle(): pl.pallas_call(functools.partial(settle_kernel, plan, loss_factor), out_s...  24 us

profile of v5, /device:TPU:97, one launch (start us, length us, event | category | flops | bytes accessed | tf_op | source)
XLA Modules:
  0.0 774.4 jit_solution(8842632741200163512)
XLA Ops:
  0.6 404.2 %stage_pipeline.1 = (f32[8,128]{1,0:T(8,128)}, bf16[3072,768]{1,0:T(8,128)(2,1)}, bf16[3072,768]{1,0:T(8,128)(2,1)}, bf16[3072,3072]{1,0:T(8,128)(2,1)}, bf16[76...) custom-call(bf16[12,256,768]{2,1,0:T(8,128)(2,1)} %bitcast.14, ...), custom_call_target="tpu_custom_call" | custom-call | flops 130459631616 | bytes 209715200 | tf_op jit(solution)/shard_map/stage_pipeline/pallas_call | solution.py:596
  404.8 345.5 %gradient_sums.1 = (f32[8,128]{1,0:T(8,128)}, f32[768,768]{1,0:T(8,128)}, f32[2304,768]{1,0:T(8,128)}, f32[3072,768]{1,0:T(8,128)}, f32[768,3072]{1,0:T(8,128)}, /*index=5*/bf16[12,256,768]{2,1,0:T(8,128)(2,1)}) custom-call(f32[8,128]{1,0:T(8,128)} %get-tuple-element.28.loss_hbm, ...), custom_call_target="tpu_custom_call", output_to_operand_aliasing={{5}: (9, {})} | custom-call | flops 43486543872 | bytes 157286400 | tf_op jit(solution)/shard_map/gradient_sums/pallas_call | solution.py:951
  750.3 24.0 %settle_results.1 = (f32[1]{0:T(128)}, f32[768,768]{1,0:T(8,128)}, f32[2304,768]{1,0:T(8,128)}, f32[3072,768]{1,0:T(8,128)}, f32[768,3072]{1,0:T(8,128)}, /*index=5*/bf16[12,256,768]{2,1,0:T(8,128)(2,1)}) custom-call(f32[8,128]{1,0:T(8,128)} %get-tuple-element.38.loss_in, f32[768,768]{1,0:T(8,128)} %get-tuple-element.39.refs_0_, ...), custom_call_target="tpu_custom_call" | custom-call | tf_op jit(solution)/shard_map/settle_results/pallas_call | solution.py:990
